TPU v7x, 32 devices: a whole 2x2x4 slice. The times are simulated.
32 devices in a mesh: fsdp: 8 (over z, x), dp: 4 (over y, core).
Axes of the slice: x: 2, y: 2, z: 4, core: 2. Of those that a mesh axis runs over, the one named last changes fastest.
Arguments:
- layer_in: bfloat16 [20480, 768], P(('fsdp', 'dp')), may hold values from -6 to 6
- ln1_gain: bfloat16 [768], P('fsdp'), may hold values from 0.5 to 1.5
- ln1_bias: bfloat16 [768], P('fsdp'), may hold values from -1.5 to 1.5
- qkv_weight: bfloat16 [768, 2304], P('fsdp'), may hold values from -0.21875 to 0.21875
- qkv_bias: bfloat16 [2304], P('fsdp'), may hold values from -1.5 to 1.5
- rope_freqs: bfloat16 [768], P('fsdp'), may hold values from -3 to 3
- out_weight: bfloat16 [768, 768], P('fsdp'), may hold values from -1.75 to 1.75
- out_bias: bfloat16 [768], P('fsdp'), may hold values from -1.5 to 1.5
- ln2_gain: bfloat16 [768], P('fsdp'), may hold values from 0.5 to 1.5
- ln2_bias: bfloat16 [768], P('fsdp'), may hold values from -1.5 to 1.5
- fc1_weight: bfloat16 [768, 3072], P('fsdp'), may hold values from -0.21875 to 0.21875
- fc1_bias: bfloat16 [3072], P('fsdp'), may hold values from -1.5 to 1.5
- fc2_weight: bfloat16 [3072, 768], P('fsdp'), may hold values from -0.109375 to 0.109375
- fc2_bias: bfloat16 [768], P('fsdp'), may hold values from -1.5 to 1.5
- image_of: int32 [20480], P(('fsdp', 'dp')), may hold values from 0 to 127, as said below
- patch_row: int32 [20480], P(('fsdp', 'dp')), may hold values from 0 to 23, as said below
- patch_col: int32 [20480], P(('fsdp', 'dp')), may hold values from 0 to 23
- grad_out: bfloat16 [20480, 768], P(('fsdp', 'dp')), may hold values from -6 to 6
Outputs:
- output: bfloat16 [20480, 768], P(('fsdp', 'dp'))
- grad_x: bfloat16 [20480, 768], P(('fsdp', 'dp'))
- grad_ln1_gain: float32 [768], P('fsdp')
- grad_ln1_bias: float32 [768], P('fsdp')
- grad_qkv_weight: float32 [768, 2304], P('fsdp')
- grad_qkv_bias: float32 [2304], P('fsdp')
- grad_rope_freqs: float32 [768], P('fsdp')
- grad_out_weight: float32 [768, 768], P('fsdp')
- grad_out_bias: float32 [768], P('fsdp')
- grad_ln2_gain: float32 [768], P('fsdp')
- grad_ln2_bias: float32 [768], P('fsdp')
- grad_fc1_weight: float32 [768, 3072], P('fsdp')
- grad_fc1_bias: float32 [3072], P('fsdp')
- grad_fc2_weight: float32 [3072, 768], P('fsdp')
- grad_fc2_bias: float32 [768], P('fsdp')
Inputs may be any that keep to these rules, and one draw needn't show every extreme that they name: `image_of`: rows with equal values form one image of 14 x 14, 20 x 20 or 24 x 24 patches, or the filler at the end of one device's rows; they stand in consecutive rows of one device. `patch_row`: an image's patches run row by row through its grid.
All inputs are finite; a program needn't handle non-finite values.
Results may differ from a plain program's by a relative error of at most 0.012.
Values may be sent and summed in bfloat16 or wider, within the bound.
A program may use at most 192 MiB of HBM per device.

v0:
```python
from functools import partial

import jax
import jax.numpy as jnp
from jax import lax
from jax.sharding import PartitionSpec as P

D = 768
H = 12
HD = 64


EPSILON = 1e-06
MASKED = -1e30


def normed(values, scales, shifts):
    centre = values - jnp.mean(values, axis=-1, keepdims=True)
    spread = jnp.mean(centre * centre, axis=-1, keepdims=True)
    return centre * lax.rsqrt(spread + EPSILON) * scales + shifts


def rotate(queries, keys_in, frequency, row_pos, col_pos):
    half_dim = queries.shape[-1] // 2
    head_count = queries.shape[1]
    split_at = head_count * half_dim
    along_col = frequency[:split_at].reshape(head_count, half_dim)
    along_row = frequency[split_at:].reshape(head_count, half_dim)
    angles = col_pos[:, None, None] * along_col[None] + row_pos[:, None, None] * along_row[None]
    cosine = jnp.cos(angles)
    sine_part = jnp.sin(angles)

    def turned(operand):
        first_half = operand[..., :half_dim]
        second_half = operand[..., half_dim:]
        return jnp.concatenate(
            [
                first_half * cosine - second_half * sine_part,
                first_half * sine_part + second_half * cosine,
            ],
            axis=-1,
        )

    return (turned(queries), turned(keys_in))


def body(
    layer_in,
    ln1_gain,
    ln1_bias,
    qkv_weight,
    qkv_bias,
    rope_freqs,
    out_weight,
    out_bias,
    ln2_gain,
    ln2_bias,
    fc1_weight,
    fc1_bias,
    fc2_weight,
    fc2_bias,
    image_of,
    patch_row,
    patch_col,
    grad_out,
):
    gathered = (
        lax.all_gather(ln1_gain, "fsdp", axis=0, tiled=True),
        lax.all_gather(ln1_bias, "fsdp", axis=0, tiled=True),
        lax.all_gather(qkv_weight, "fsdp", axis=0, tiled=True),
        lax.all_gather(qkv_bias, "fsdp", axis=0, tiled=True),
        lax.all_gather(rope_freqs, "fsdp", axis=0, tiled=True),
        lax.all_gather(out_weight, "fsdp", axis=0, tiled=True),
        lax.all_gather(out_bias, "fsdp", axis=0, tiled=True),
        lax.all_gather(ln2_gain, "fsdp", axis=0, tiled=True),
        lax.all_gather(ln2_bias, "fsdp", axis=0, tiled=True),
        lax.all_gather(fc1_weight, "fsdp", axis=0, tiled=True),
        lax.all_gather(fc1_bias, "fsdp", axis=0, tiled=True),
        lax.all_gather(fc2_weight, "fsdp", axis=0, tiled=True),
        lax.all_gather(fc2_bias, "fsdp", axis=0, tiled=True),
    )
    (
        gain_one,
        shift_one,
        qkv_mat,
        qkv_shift,
        frequency,
        out_mat,
        out_shift,
        gain_two,
        shift_two,
        fc1_mat,
        fc1_shift,
        fc2_mat,
        fc2_shift,
    ) = gathered
    token_count = layer_in.shape[0]
    inputs = layer_in.astype(jnp.float32)
    row_pos = patch_row.astype(jnp.float32)
    col_pos = patch_col.astype(jnp.float32)
    scale_qk = HD ** (-0.5)
    same_image = image_of[:, None] == image_of[None, :]
    normed_one, norm_one_pull = jax.vjp(
        normed, inputs, gain_one.astype(jnp.float32), shift_one.astype(jnp.float32)
    )
    normed_one_low = normed_one.astype(jnp.bfloat16)
    projected = jnp.dot(
        normed_one_low, qkv_mat, preferred_element_type=jnp.float32
    ) + qkv_shift.astype(jnp.float32)
    queries = projected[:, :D].reshape(token_count, H, HD)
    keys_in = projected[:, D : 2 * D].reshape(token_count, H, HD)
    values_in = projected[:, 2 * D :].reshape(token_count, H, HD)
    rotation = partial(rotate, row_pos=row_pos, col_pos=col_pos)
    (query_rot, key_rot), rope_pull = jax.vjp(
        rotation, queries, keys_in, frequency.astype(jnp.float32)
    )
    query_heads = query_rot.astype(jnp.bfloat16).transpose(1, 0, 2)
    key_heads = key_rot.astype(jnp.bfloat16).transpose(1, 0, 2)
    value_heads = values_in.astype(jnp.bfloat16).transpose(1, 0, 2)

    def head_scores(query_one, key_one):
        scores = (
            jnp.einsum("qd,kd->qk", query_one, key_one, preferred_element_type=jnp.float32)
            * scale_qk
        )
        return jnp.where(same_image, scores, MASKED)

    def head_forward(operands):
        query_one, key_one, value_one = operands
        scores = head_scores(query_one, key_one)
        peak_score = jnp.max(scores, axis=-1, keepdims=True)
        log_total = peak_score + jnp.log(
            jnp.sum(jnp.exp(scores - peak_score), axis=-1, keepdims=True)
        )
        probs = jnp.exp(scores - log_total)
        mixed_one = jnp.dot(
            probs.astype(jnp.bfloat16), value_one, preferred_element_type=jnp.float32
        )
        return (mixed_one, log_total[:, 0])

    mixed_heads, log_totals = lax.map(head_forward, (query_heads, key_heads, value_heads))
    mixed_low = mixed_heads.transpose(1, 0, 2).reshape(token_count, D).astype(jnp.bfloat16)
    middle = (
        inputs
        + jnp.dot(mixed_low, out_mat, preferred_element_type=jnp.float32)
        + out_shift.astype(jnp.float32)
    )
    normed_two, norm_two_pull = jax.vjp(
        normed, middle, gain_two.astype(jnp.float32), shift_two.astype(jnp.float32)
    )
    normed_two_low = normed_two.astype(jnp.bfloat16)
    hidden = jnp.dot(
        normed_two_low, fc1_mat, preferred_element_type=jnp.float32
    ) + fc1_shift.astype(jnp.float32)
    active, gelu_pull = jax.vjp(jax.nn.gelu, hidden)
    active_low = active.astype(jnp.bfloat16)
    result = (
        middle
        + jnp.dot(active_low, fc2_mat, preferred_element_type=jnp.float32)
        + fc2_shift.astype(jnp.float32)
    )
    output = result.astype(jnp.bfloat16)
    again = (
        lax.all_gather(ln1_gain, "fsdp", axis=0, tiled=True),
        lax.all_gather(ln1_bias, "fsdp", axis=0, tiled=True),
        lax.all_gather(qkv_weight, "fsdp", axis=0, tiled=True),
        lax.all_gather(qkv_bias, "fsdp", axis=0, tiled=True),
        lax.all_gather(rope_freqs, "fsdp", axis=0, tiled=True),
        lax.all_gather(out_weight, "fsdp", axis=0, tiled=True),
        lax.all_gather(out_bias, "fsdp", axis=0, tiled=True),
        lax.all_gather(ln2_gain, "fsdp", axis=0, tiled=True),
        lax.all_gather(ln2_bias, "fsdp", axis=0, tiled=True),
        lax.all_gather(fc1_weight, "fsdp", axis=0, tiled=True),
        lax.all_gather(fc1_bias, "fsdp", axis=0, tiled=True),
        lax.all_gather(fc2_weight, "fsdp", axis=0, tiled=True),
        lax.all_gather(fc2_bias, "fsdp", axis=0, tiled=True),
    )
    qkv_back = again[2]
    out_back = again[5]
    fc1_back = again[9]
    fc2_back = again[11]
    upstream = grad_out.astype(jnp.float32)
    grad_fc2 = jnp.einsum("ti,to->io", active_low, grad_out, preferred_element_type=jnp.float32)
    grad_fc2_shift = jnp.sum(upstream, axis=0)
    grad_active = jnp.einsum("to,io->ti", grad_out, fc2_back, preferred_element_type=jnp.float32)
    (grad_hidden,) = gelu_pull(grad_active)
    grad_hidden_low = grad_hidden.astype(jnp.bfloat16)
    grad_fc1 = jnp.einsum(
        "td,th->dh", normed_two_low, grad_hidden_low, preferred_element_type=jnp.float32
    )
    grad_fc1_shift = jnp.sum(grad_hidden_low.astype(jnp.float32), axis=0)
    grad_normed_two = jnp.einsum(
        "th,dh->td", grad_hidden_low, fc1_back, preferred_element_type=jnp.float32
    )
    grad_middle_norm, grad_gain_two, grad_shift_two = norm_two_pull(grad_normed_two)
    grad_middle = upstream + grad_middle_norm
    grad_middle_low = grad_middle.astype(jnp.bfloat16)
    grad_out_shift = jnp.sum(grad_middle_low.astype(jnp.float32), axis=0)
    grad_out_mat = jnp.einsum(
        "ti,to->io", mixed_low, grad_middle_low, preferred_element_type=jnp.float32
    )
    grad_mixed = jnp.einsum(
        "to,io->ti", grad_middle_low, out_back, preferred_element_type=jnp.float32
    )
    grad_mixed_heads = (
        grad_mixed.astype(jnp.bfloat16).reshape(token_count, H, HD).transpose(1, 0, 2)
    )

    def head_backward(operands):
        query_one, key_one, value_one, grad_one, log_total = operands
        scores = head_scores(query_one, key_one)
        probs = jnp.exp(scores - log_total[:, None])
        grad_value = jnp.einsum(
            "qk,qd->kd", probs.astype(jnp.bfloat16), grad_one, preferred_element_type=jnp.float32
        )
        grad_probs = jnp.einsum(
            "qd,kd->qk", grad_one, value_one, preferred_element_type=jnp.float32
        )
        grad_scores = probs * (grad_probs - jnp.sum(probs * grad_probs, axis=-1, keepdims=True))
        grad_scores_low = grad_scores.astype(jnp.bfloat16)
        grad_query = (
            jnp.einsum("qk,kd->qd", grad_scores_low, key_one, preferred_element_type=jnp.float32)
            * scale_qk
        )
        grad_key = (
            jnp.einsum("qk,qd->kd", grad_scores_low, query_one, preferred_element_type=jnp.float32)
            * scale_qk
        )
        return (grad_query, grad_key, grad_value)

    grad_query_heads, grad_key_heads, grad_value_heads = lax.map(
        head_backward, (query_heads, key_heads, value_heads, grad_mixed_heads, log_totals)
    )
    grad_query_rot = grad_query_heads.transpose(1, 0, 2)
    grad_key_rot = grad_key_heads.transpose(1, 0, 2)
    grad_values = grad_value_heads.transpose(1, 0, 2)
    grad_queries, grad_keys, grad_frequency = rope_pull((grad_query_rot, grad_key_rot))
    grad_projected = jnp.concatenate(
        [
            grad_queries.reshape(token_count, D),
            grad_keys.reshape(token_count, D),
            grad_values.reshape(token_count, D),
        ],
        axis=1,
    ).astype(jnp.bfloat16)
    grad_qkv_shift = jnp.sum(grad_projected.astype(jnp.float32), axis=0)
    grad_qkv = jnp.einsum(
        "td,tp->dp", normed_one_low, grad_projected, preferred_element_type=jnp.float32
    )
    grad_normed_one = jnp.einsum(
        "tp,dp->td", grad_projected, qkv_back, preferred_element_type=jnp.float32
    )
    grad_input_norm, grad_gain_one, grad_shift_one = norm_one_pull(grad_normed_one)
    grad_x = (grad_middle + grad_input_norm).astype(jnp.bfloat16)
    owned = (
        lax.psum_scatter(grad_gain_one, "fsdp", scatter_dimension=0, tiled=True),
        lax.psum_scatter(grad_shift_one, "fsdp", scatter_dimension=0, tiled=True),
        lax.psum_scatter(grad_qkv, "fsdp", scatter_dimension=0, tiled=True),
        lax.psum_scatter(grad_qkv_shift, "fsdp", scatter_dimension=0, tiled=True),
        lax.psum_scatter(grad_frequency, "fsdp", scatter_dimension=0, tiled=True),
        lax.psum_scatter(grad_out_mat, "fsdp", scatter_dimension=0, tiled=True),
        lax.psum_scatter(grad_out_shift, "fsdp", scatter_dimension=0, tiled=True),
        lax.psum_scatter(grad_gain_two, "fsdp", scatter_dimension=0, tiled=True),
        lax.psum_scatter(grad_shift_two, "fsdp", scatter_dimension=0, tiled=True),
        lax.psum_scatter(grad_fc1, "fsdp", scatter_dimension=0, tiled=True),
        lax.psum_scatter(grad_fc1_shift, "fsdp", scatter_dimension=0, tiled=True),
        lax.psum_scatter(grad_fc2, "fsdp", scatter_dimension=0, tiled=True),
        lax.psum_scatter(grad_fc2_shift, "fsdp", scatter_dimension=0, tiled=True),
    )
    summed = lax.psum(
        (
            owned[0],
            owned[1],
            owned[2],
            owned[3],
            owned[4],
            owned[5],
            owned[6],
            owned[7],
            owned[8],
            owned[9],
            owned[10],
            owned[11],
            owned[12],
        ),
        "dp",
    )
    return (
        output,
        grad_x,
        summed[0],
        summed[1],
        summed[2],
        summed[3],
        summed[4],
        summed[5],
        summed[6],
        summed[7],
        summed[8],
        summed[9],
        summed[10],
        summed[11],
        summed[12],
    )


def solution(mesh):
    in_specs = (
        P(("fsdp", "dp"), None),
        P("fsdp"),
        P("fsdp"),
        P("fsdp", None),
        P("fsdp"),
        P("fsdp"),
        P("fsdp", None),
        P("fsdp"),
        P("fsdp"),
        P("fsdp"),
        P("fsdp", None),
        P("fsdp"),
        P("fsdp", None),
        P("fsdp"),
        P(("fsdp", "dp")),
        P(("fsdp", "dp")),
        P(("fsdp", "dp")),
        P(("fsdp", "dp"), None),
    )
    out_specs = (
        P(("fsdp", "dp"), None),
        P(("fsdp", "dp"), None),
        P("fsdp"),
        P("fsdp"),
        P("fsdp", None),
        P("fsdp"),
        P("fsdp"),
        P("fsdp", None),
        P("fsdp"),
        P("fsdp"),
        P("fsdp"),
        P("fsdp", None),
        P("fsdp"),
        P("fsdp", None),
        P("fsdp"),
    )
    return jax.shard_map(body, mesh=mesh, in_specs=in_specs, out_specs=out_specs, check_vma=False)
```

profile of v0, /device:TPU:0, one launch (start us, length us, event | category | flops | bytes accessed | tf_op | source)
XLA Modules:
  0.0 979.9 jit_solution(2736327719960021424)
XLA Ops:
  14.3 40.4 %all-reduce.26 = (bf16[2304]{0:T(1024)(128)(2,1)S(1)}, bf16[768]{0:T(1024)(128)(2,1)S(1)}, bf16[768]{0:T(1024)(128)(2,1)S(1)}, bf16[768]{0:T(1024)(128)(2,1)S(1)...) all-reduce(bf16[2304]{0:T(1024)(128)(2,1)S(1)} %dynamic-update-slic, ...), channel_id=1, replica_groups=mesh['fsdp'=8,'dp'=4] {'fsdp'}, use_global_device_ids=true, to_apply=%add.8 | all-reduce | flops 7680 | bytes 30720
  56.5 26.7 %all-gather = bf16[8,1,384]{2,1,0:T(2,128)(2,1)S(1)} all-gather(bf16[1,1,384]{2,1,0:T(2,128)(2,1)S(1)} %reshape.222), channel_id=1, replica_groups=mesh['fsdp'=8,'dp'=4] {'fsdp'}, dimensions={0}, use_global_device_ids=true | all-gather | bytes 6912 | tf_op jit(solution)/shard_map/all_gather | solution.py:78
  83.2 4.7 convolution_add_fusion
  93.2 2.9 copy.54
  96.0 6.9 subtract_convert_fusion
  104.5 2.7 copy.57
  107.2 2.7 copy.58
  112.1 2.7 copy.59
  114.9 44.6 %while.30 = (s32[]{:T(128)}, bf16[12,640,64]{1,2,0:T(8,128)(2,1)}, f32[12,640]{1,0:T(8,128)S(1)}, bf16[12,640,64]{2,1,0:T(8,128)(2,1)}, bf16[12,640,64]{2,1,0:T(...) while((s32[]{:T(128)}, bf16[12,640,64]{1,2,0:T(8,128)(2,1)}, ...), condition=%wide.region_5.6_spmd.clone.clone, body=%wide.region_2.5_spmd.clone.sunk.clone | while | flops 108133760 | bytes 5609049 | solution.py:141
  159.5 2.7 fusion.81
  163.8 36.8 %all-gather.10.cloned.1.call-done = bf16[768,3072]{1,0:T(8,128)(2,1)} async-done(((bf16[96,3072]{1,0:T(8,128)(2,1)}), bf16[768,3072]{1,0:T(8,128)(2,1)}) %all-gather.10.cloned.1.call-update) | async-done | bytes 4718608 | tf_op jit(solution)/shard_map/all_gather | solution.py:77
  200.6 9.4 fusion.70
  210.0 70.3 %all-gather.12.cloned.1.call-done = bf16[3072,768]{1,0:T(8,128)(2,1)} async-done(((bf16[384,768]{1,0:T(8,128)(2,1)}), bf16[3072,768]{1,0:T(8,128)(2,1)}) %all-gather.12.cloned.1.call-update) | async-done | bytes 4718608 | tf_op jit(solution)/shard_map/all_gather | solution.py:79
  280.3 11.6 %convert_reduce_fusion = (f32[3072]{0:T(1024)S(1)}, bf16[640,3072]{1,0:T(8,128)(2,1)S(1)}) fusion(f32[640,3072]{1,0:T(8,128)} %fusion.70, f32[3072]{0:T(1024)S(1)} %bitcast.165, bf16[640,768]{1,0:T(8,128)(2,1)} %param.39, bf16[3072,768]{1,0:T(8,128)(2,1)} %all-gather.12.cloned.1.call-done), kind=kOutput, calls=%fused_computation.59 | convolution fusion | flops 3065115648 | bytes 17522688 | tf_op jit(solution)/shard_map/to,io->ti/dot_general | solution.py:185
  292.0 3.6 multiply_reduce_fusion.1
  298.6 2.5 fusion.82
  301.2 3.5 convolution_convert_fusion
  306.9 107.4 %while.31 = (s32[]{:T(128)}, f32[12,640,64]{1,2,0:T(8,128)}, f32[12,640,64]{1,2,0:T(8,128)}, bf16[12,640,64]{1,2,0:T(8,128)(2,1)}, bf16[12,640,64]{2,1,0:T(8,128...) while((s32[]{:T(128)}, f32[12,640,64]{1,2,0:T(8,128)}, ...), condition=%wide.region_12.13_spmd.clone.clone, body=%wide.region_10.12_spmd.clone.sunk.clone | while | flops 266321280 | bytes 13790321 | solution.py:231
  414.4 7.4 multiply_add_fusion
  421.8 4.0 multiply_reduce_fusion.5
  427.8 6.2 fusion.64
  435.5 8.6 fusion.69
  445.3 12.2 %fusion.71 = f32[3072,768]{1,0:T(8,128)} fusion(bf16[640,768]{1,0:T(8,128)(2,1)S(1)} %copy-done.16, f32[640,3072]{1,0:T(8,128)} %fusion.70, f32[3072]{0:T(1024)S(1)} %bitcast.166), kind=kOutput, calls=%fused_computation.127 | convolution fusion | flops 3039559680 | bytes 18296832 | tf_op jit(solution)/shard_map/ti,to->io/dot_general | solution.py:183
  461.6 4.9 fusion.72
  468.9 92.8 %reduce-scatter.5.cloned.1.call-done = f32[96,2304]{1,0:T(8,128)} async-done(((f32[768,2304]{1,0:T(8,128)}), f32[96,2304]{1,0:T(8,128)}) %reduce-scatter.5.cloned.1.call-update) | async-done | bytes 884752 | tf_op jit(solution)/shard_map/reduce_scatter | solution.py:258
  561.7 164.9 %reduce-scatter.9.cloned.1.call-done = f32[96,3072]{1,0:T(8,128)} async-done(((f32[768,3072]{1,0:T(8,128)}), f32[96,3072]{1,0:T(8,128)}) %reduce-scatter.9.cloned.1.call-update) | async-done | bytes 1179664 | tf_op jit(solution)/shard_map/reduce_scatter | solution.py:265
  726.6 164.8 %reduce-scatter.11.cloned.1.call-done = f32[384,768]{1,0:T(8,128)} async-done(((f32[3072,768]{1,0:T(8,128)}), f32[384,768]{1,0:T(8,128)}) %reduce-scatter.11.cloned.1.call-update) | async-done | bytes 1179664 | tf_op jit(solution)/shard_map/reduce_scatter | solution.py:267
  891.4 3.2 convert_reduce_fusion.3
  894.7 35.7 %all-reduce.23 = (f32[768]{0:T(1024)S(1)}, f32[768]{0:T(1024)S(1)}, f32[2304]{0:T(1024)S(1)}, f32[768]{0:T(1024)S(1)}, f32[768]{0:T(1024)S(1)}, /*index=5*/f32[7...) all-reduce(f32[768]{0:T(1024)S(1)} %get-tuple-element.205, ...), channel_id=2, replica_groups=mesh['fsdp'=8,'dp'=4] {'fsdp'}, use_global_device_ids=true, to_apply=%region_16.17.clone | all-reduce | flops 10752 | bytes 86016
  931.1 6.5 all-reduce.24
  937.6 11.5 %add_convert_fusion.3 = bf16[640,768]{1,0:T(8,128)(2,1)} fusion(f32[640,768]{1,0:T(8,128)} %copy-done.2, bf16[3072,768]{1,0:T(8,128)(2,1)} %all-gather.12.cloned.1.call-done, f32[768]{0:T(1024)S(1)} %convert_element_type.115, f32[640,3072]{1,0:T(8,128)} %fusion.70, f32[3072]{0:T(1024)S(1)} %bitcast.167), kind=kOutput, calls=%fused_computation.90 | convolution fusion | flops 3041034240 | bytes 15547392 | tf_op jit(solution)/shard_map/dot_general | solution.py:159
  949.1 19.0 %all-reduce.29.cloned.1.call-done = (f32[96,2304]{1,0:T(8,128)}, f32[96,768]{1,0:T(8,128)}, f32[96,3072]{1,0:T(8,128)}, f32[384,768]{1,0:T(8,128)}) async-done(((f32[96,2304]{1,0:T(8,128)}, f32[96,768]{1,0:T(8,128)}, f32[96,3072]{1,0:T(8,128)}, f32[384,768]{1,0:T(8,128)}), (f32[96,2304]{1,0:T(8,128)}, f32[96,768]{1,0:T(8,128)}, f32[96,3072]{1,0:T(8,128)}, ...) | async-done | bytes 3538960 | tf_op jit(solution)/shard_map/psum | solution.py:270
  (326 shorter events, 189.5 us)
Async XLA Ops:
  7.2 3.1 copy-start.26
  7.2 5.1 copy-start.30
  7.2 5.4 copy-start.31
  7.2 5.6 copy-start.32
  7.2 5.8 copy-start.33
  7.2 6.1 copy-start.34
  7.2 6.3 copy-start.35
  7.3 6.5 copy-start.36
  7.3 6.7 copy-start.27
  7.3 76.0 %all-gather.6.cloned.1.call-start = ((), (), s32[]{:S(2)}) async-start(), calls=%async_computation.4 | async-start | bytes 3981312 | tf_op jit(solution)/shard_map/all_gather | solution.py:70
  8.0 151.5 %all-gather.8.cloned.1.call-start = ((), (), s32[]{:S(2)}) async-start(), calls=%async_computation.5 | async-start | bytes 1327104 | tf_op jit(solution)/shard_map/all_gather | solution.py:73
  8.8 191.8 %all-gather.10.cloned.1.call-start = ((), (), s32[]{:S(2)}) async-start(), calls=%async_computation.6 | async-start | bytes 5308416 | tf_op jit(solution)/shard_map/all_gather | solution.py:77
  9.5 46.2 %copy-start.5 = (bf16[640,768]{1,0:T(8,128)(2,1)S(1)}, bf16[640,768]{1,0:T(8,128)(2,1)}, u32[]{:S(2)}) copy-start(bf16[640,768]{1,0:T(8,128)(2,1)} %param.22) | copy-start | bytes 2949124
  9.5 270.8 %all-gather.12.cloned.1.call-start = ((), (), s32[]{:S(2)}) async-start(), calls=%async_computation.7 | async-start | bytes 5308416 | tf_op jit(solution)/shard_map/all_gather | solution.py:79
  10.1 458.8 %reduce-scatter.7.cloned.1.call-start = ((), (), s32[]{:S(2)}) async-start(), calls=%async_computation.9 | async-start | bytes 2654208 | tf_op jit(solution)/shard_map/reduce_scatter | solution.py:261
  10.2 77.7 %copy-start.6 = (bf16[12,640,64]{1,2,0:T(8,128)(2,1)}, bf16[12,640,64]{1,2,0:T(8,128)(2,1)S(1)}, u32[]{:S(2)}) copy-start(bf16[12,640,64]{1,2,0:T(8,128)(2,1)S(1)} %fusion.78) | copy-start | bytes 2949124
  112.1 2.7 copy-start.22
  280.3 11.6 %copy-start.3 = (f32[640,768]{1,0:T(8,128)S(1)}, f32[640,768]{1,0:T(8,128)}, u32[]{:S(2)}) copy-start(f32[640,768]{1,0:T(8,128)} %copy-done.2) | copy-start | bytes 5898244
  280.3 11.6 %copy-start.29 = (bf16[768,3072]{1,0:T(8,128)(2,1)S(1)}, bf16[768,3072]{1,0:T(8,128)(2,1)}, u32[]{:S(2)}) copy-start(bf16[768,3072]{1,0:T(8,128)(2,1)} %all-gather.10.cloned.1.call-done) | copy-start | bytes 14155780
  291.9 3.6 copy-start.17
  306.9 254.8 %reduce-scatter.5.cloned.1.call-start = ((), (), s32[]{:S(2)}) async-start(), calls=%async_computation.8 | async-start | bytes 7962624 | tf_op jit(solution)/shard_map/reduce_scatter | solution.py:258
  414.4 7.4 copy-start.9
  425.9 1.9 copy-start.7
  434.0 292.6 %reduce-scatter.9.cloned.1.call-start = ((), (), s32[]{:S(2)}) async-start(), calls=%async_computation.10 | async-start | bytes 10616832 | tf_op jit(solution)/shard_map/reduce_scatter | solution.py:265
  444.2 447.2 %reduce-scatter.11.cloned.1.call-start = ((), (), s32[]{:S(2)}) async-start(), calls=%async_computation.11 | async-start | bytes 10616832 | tf_op jit(solution)/shard_map/reduce_scatter | solution.py:267
  457.5 2.3 copy-start.8
  457.5 2.3 copy-start.12
  457.5 510.5 %all-reduce.29.cloned.1.call-start = ((), (), s32[]{:S(2)}) async-start(), calls=%async_computation.12 | async-start | bytes 7077888 | tf_op jit(solution)/shard_map/psum | solution.py:270
  468.8 422.6 %copy-start.1 = (f32[640,768]{1,0:T(8,128)S(1)}, f32[640,768]{1,0:T(8,128)}, u32[]{:S(2)}) copy-start(f32[640,768]{1,0:T(8,128)} %copy-done) | copy-start | bytes 5898244
  968.1 2.3 copy-start.23
  968.1 3.0 copy-start.19
  968.1 4.0 copy-start.18
  (14 other events, 19.8 us)
Sparse Core Ops, SparseCore 0:
  10.3 67.8 all-gather.5
  80.4 39.9 all-gather.7
  122.5 78.0 all-gather.9
  202.6 77.6 all-gather.11
  307.0 67.8 reduce-scatter.6
  434.1 127.5 reduce-scatter.4
  565.3 161.2 reduce-scatter.8
  730.2 161.1 reduce-scatter.10
  894.0 74.0 all-reduce.28
where the time goes:
time: 988 us; the launch traced here: 980 us
  waiting for transfers between devices  551 us (56%)
  matrix products  226 us (23%)
  blocking collectives  109 us (11%)
  local copies, waits for them, and re-layouts  39.8 us (4%)
  other arithmetic  33.9 us (3%)
  between operations  18 us (2%)
    reduce_scatter x1, waiting for transfers between devices, body(): lax.psum_scatter(grad_fc1, 'fsdp', scatter_dimension=0, tiled=True)  165 us
    reduce_scatter x1, waiting for transfers between devices, body(): lax.psum_scatter(grad_fc2, 'fsdp', scatter_dimension=0, tiled=True)  165 us
    reduce_scatter x1, waiting for transfers between devices, body(): lax.psum_scatter(grad_qkv, 'fsdp', scatter_dimension=0, tiled=True)  92.8 us
    unnamed x2, blocking collectives  76.2 us
    all_gather x1, waiting for transfers between devices, body(): lax.all_gather(fc2_weight, 'fsdp', axis=0, tiled=True)  70.3 us
    all_gather x1, waiting for transfers between devices, body(): lax.all_gather(fc1_weight, 'fsdp', axis=0, tiled=True)  36.8 us
    dot_general x24, matrix products, head_scores(): jnp.einsum('qd,kd->qk', query_one, key_one, preferred_element_type=jnp.fl...  36.7 us
    all_gather x1, blocking collectives, body(): lax.all_gather(fc1_bias, 'fsdp', axis=0, tiled=True)  26.7 us
  transfers between devices with their start and end apart: 9, of which 6 were waited for; matrix products, arithmetic and copies ran while one was open for 27% of the time, Pallas kernels for 0%

commit v1 on v0

--- a/solution.py
+++ b/solution.py
@@ -1,17 +1,1074 @@
+import math
 from functools import partial
 
 import jax
 import jax.numpy as jnp
 from jax import lax
+from jax.experimental import pallas as pl
+from jax.experimental.pallas import tpu as pltpu
 from jax.sharding import PartitionSpec as P
 
 D = 768
 H = 12
 HD = 64
-
-
 EPSILON = 1e-06
 MASKED = -1e30
+
+MESH = pl.DeviceIdType.MESH
+
+
+def position(index, count):
+    odd = lax.rem(index, 2)
+    half = lax.div(index, 2)
+    return (1 - odd) * half + odd * (count - 1 - half)
+
+
+def member(place, count):
+    place = lax.rem(place + 2 * count, count)
+    back = lax.div(place, count // 2)
+    return (1 - back) * 2 * place + back * (2 * (count - 1 - place) + 1)
+
+
+class Place:
+    def __init__(self, count):
+        self.count = count
+        self.far = count // 2
+        self.fsdp = lax.axis_index("fsdp")
+        self.dp = lax.axis_index("dp")
+        self.plane = lax.div(self.dp, 2)
+        self.core = lax.rem(self.dp, 2)
+        self.place = position(self.fsdp, count)
+        self.ring = (
+            (member(self.place + 1, count), self.dp),
+            (member(self.place - 1, count), self.dp),
+        )
+        self.across = (self.fsdp, (1 - self.plane) * 2 + self.core)
+        self.twin = (self.fsdp, self.plane * 2 + 1 - self.core)
+
+    def owner(self, direction, step):
+        return member(self.place - step if direction == 0 else self.place + step, self.count)
+
+    def greet(self, peers=None):
+        barrier = pltpu.get_barrier_semaphore()
+        partners = tuple(self.ring if peers is None else peers) + (self.across, self.twin)
+        for device in partners:
+            pl.semaphore_signal(barrier, inc=1, device_id=device, device_id_type=MESH)
+        pl.semaphore_wait(barrier, len(partners))
+
+
+class Sems:
+    def __init__(self, send, recv):
+        self.send, self.recv, self.used = send, recv, 0
+
+    def take(self):
+        self.used += 1
+        return self.send.at[self.used - 1], self.recv.at[self.used - 1]
+
+
+def remote(src, dst, sems, device):
+    return pltpu.make_async_remote_copy(
+        src_ref=src, dst_ref=dst, send_sem=sems[0], recv_sem=sems[1], device_id=device, device_id_type=MESH
+    )
+
+
+def rows_at(start, size, unit=16):
+    return pl.ds(pl.multiple_of(start, unit), size)
+
+
+class Gather:
+    def __init__(self, where, sems, shard, full, shared, local_sem):
+        self.where, self.shard, self.full, self.shared = where, shard, full, shared
+        self.rows, self.columns = shard.shape
+        self.ring_rows = self.rows - shared
+        self.cut = -(-max(self.ring_rows // 2, shared) // 16) * 16
+        self.local = pltpu.make_async_copy(
+            shard, full.at[rows_at(where.fsdp * self.rows, self.rows)], local_sem
+        )
+        far = where.far
+        take = sems.take
+        self.ring_sems = [[take() for _ in range(far)] for _ in range(2)]
+        self.across_sems = [[take() for _ in range(far)] for _ in range(2)]
+        self.twin_sems = [[take() for _ in range(far)] for _ in range(2)]
+        self.twin_across_sems = [[take() for _ in range(far)] for _ in range(2)]
+        self.build()
+
+    def columns_of(self, core):
+        half = self.columns // 2
+        return pl.ds(pl.multiple_of(core * half, 128), half)
+
+    def ring_span(self, direction, step):
+        start, size = 0, self.ring_rows
+        if step == self.where.far:
+            start, size = (0, self.cut) if direction == 0 else (self.cut, self.ring_rows - self.cut)
+        return start, size
+
+    def ring_view(self, owner, direction, step, core, ref=None):
+        start, size = self.ring_span(direction, step)
+        start = start + self.where.plane * self.shared
+        if ref is None:
+            ref, start = self.full, start + owner * self.rows
+        return ref.at[rows_at(start, size), self.columns_of(core)]
+
+    def across_view(self, owner, plane, core):
+        start = owner * self.rows + plane * (self.rows - self.shared)
+        return self.full.at[rows_at(start, self.shared), self.columns_of(core)]
+
+    def build(self):
+        where, far = self.where, self.where.far
+        near = range(1, far + 1)
+        self.ring_out, self.ring_in, self.across_out, self.across_in = {}, {}, {}, {}
+        self.twin_out, self.twin_in, self.twin_across_out, self.twin_across_in = {}, {}, {}, {}
+        for direction in range(2):
+            to = where.ring[direction]
+            src = self.ring_view(None, direction, 1, where.core, self.shard)
+            dst = self.ring_view(where.fsdp, direction, 1, where.core)
+            self.ring_out[direction, 1] = remote(src, dst, self.ring_sems[direction][0], to)
+            for step in near:
+                owner = where.owner(direction, step)
+                view = self.ring_view(owner, direction, step, where.core)
+                self.ring_in[direction, step] = remote(view, view, self.ring_sems[direction][step - 1], to)
+                sems = self.twin_sems[direction][step - 1]
+                self.twin_out[direction, step] = remote(view, view, sems, where.twin)
+                view = self.ring_view(owner, direction, step, 1 - where.core)
+                self.twin_in[direction, step] = remote(view, view, sems, where.twin)
+                if step < far:
+                    view = self.ring_view(owner, direction, step + 1, where.core)
+                    self.ring_out[direction, step + 1] = remote(view, view, self.ring_sems[direction][step], to)
+                if step < far or direction == 0:
+                    sems = self.across_sems[direction][step - 1]
+                    view = self.across_view(owner, where.plane, where.core)
+                    self.across_out[direction, step] = remote(view, view, sems, where.across)
+                    view = self.across_view(owner, 1 - where.plane, where.core)
+                    self.across_in[direction, step] = remote(view, view, sems, where.across)
+                    sems = self.twin_across_sems[direction][step - 1]
+                    self.twin_across_out[direction, step] = remote(view, view, sems, where.twin)
+                    view = self.across_view(owner, 1 - where.plane, 1 - where.core)
+                    self.twin_across_in[direction, step] = remote(view, view, sems, where.twin)
+
+    def start(self):
+        self.local.start()
+        for direction in range(2):
+            self.ring_out[direction, 1].start()
+
+    def ring_step(self, step):
+        far = self.where.far
+        for direction in range(2):
+            self.ring_in[direction, step].wait_recv()
+            if step < far:
+                self.ring_out[direction, step + 1].start()
+                self.across_out[direction, step].start()
+            self.twin_out[direction, step].start()
+        if step == far:
+            self.across_out[0, step].start()
+
+    def across_step(self, step):
+        for direction in range(2 if step < self.where.far else 1):
+            self.across_in[direction, step].wait_recv()
+            self.twin_across_out[direction, step].start()
+
+    def tick(self, step):
+        if step <= self.where.far:
+            self.ring_step(step)
+        if step > 1:
+            self.across_step(step - 1)
+
+    def finish(self):
+        for table in (self.twin_in, self.twin_across_in):
+            for copy in table.values():
+                copy.wait_recv()
+        self.local.wait()
+
+    def drain(self):
+        for table in (self.ring_out, self.across_out, self.twin_out, self.twin_across_out):
+            for copy in table.values():
+                copy.wait_send()
+
+
+class Reduce:
+    def __init__(self, where, sems, grad, out, shared, bufs):
+        self.where, self.grad, self.out, self.shared = where, grad, out, shared
+        self.pair, self.other, self.passing, self.final = bufs
+        self.rows = self.pair.shape[0] // where.count
+        self.half = self.pair.shape[1]
+        self.ring_rows = self.rows - shared
+        self.cut = -(-max(self.ring_rows // 2, shared) // 16) * 16
+        far, count = where.far, where.count
+        order = [(0, far)] + [(d, j) for j in range(far - 1, 0, -1) for d in range(2)] + [(0, 0)]
+        self.owners = [self.target(*o) for o in order]
+        theirs, mine = self.columns_of(1 - where.core), self.columns_of(where.core)
+        self.mine = mine
+        self.pair_out, self.other_out, self.other_in, self.ring_out, self.ring_in = [], [], [], {}, {}
+        for owner in self.owners:
+            rows = rows_at(owner * self.rows, self.rows)
+            self.pair_out.append(remote(grad.at[rows, theirs], self.pair.at[rows], sems.take(), where.twin))
+            give = rows_at(owner * self.rows + (1 - where.plane) * self.ring_rows, shared)
+            came = self.other.at[rows_at(owner * shared, shared)]
+            take = sems.take()
+            self.other_out.append(remote(self.pair.at[give], came, take, where.across))
+            self.other_in.append(remote(came, came, take, where.across))
+        for direction in range(2):
+            to = where.ring[direction]
+            for step in range(1, far + 1):
+                start, size = self.span(direction, step)
+                rows = self.ring_rows_of(self.target(direction, far + 1 - step), start, size)
+                came = self.passing.at[direction, step - 1, pl.ds(start, size)]
+                take = sems.take()
+                self.ring_out[direction, step] = remote(self.pair.at[rows], came, take, to)
+                self.ring_in[direction, step] = remote(came, came, take, to)
+        self.own = self.ring_rows_of(where.fsdp, 0, self.ring_rows)
+        take = sems.take()
+        self.final_out = remote(self.pair.at[self.own], self.final, take, where.across)
+        self.final_in = remote(self.final, self.final, take, where.across)
+        take = sems.take()
+        given, taken = out.at[:, mine], out.at[:, theirs]
+        self.out_out = remote(given, given, take, where.twin)
+        self.out_in = remote(taken, taken, take, where.twin)
+
+    @staticmethod
+    def shapes(rows, columns, count, shared):
+        half, ring_rows = columns // 2, rows - shared
+        return [
+            pltpu.VMEM((count * rows, half), jnp.bfloat16),
+            pltpu.VMEM((count * shared, half), jnp.bfloat16),
+            pltpu.VMEM((2, count // 2, ring_rows, half), jnp.bfloat16),
+            pltpu.VMEM((ring_rows, half), jnp.bfloat16),
+        ]
+
+    @staticmethod
+    def copies(count):
+        return 2 * count + 2 * (count // 2) + 2
+
+    def target(self, direction, distance):
+        return self.where.owner(1 - direction, distance)
+
+    def columns_of(self, core):
+        return pl.ds(pl.multiple_of(core * self.half, 128), self.half)
+
+    def span(self, direction, step):
+        if step > 1:
+            return 0, self.ring_rows
+        return (0, self.cut) if direction == 0 else (self.cut, self.ring_rows - self.cut)
+
+    def ring_rows_of(self, owner, start, size):
+        return rows_at(owner * self.rows + self.where.plane * self.shared + start, size)
+
+    def start(self):
+        for copy in self.pair_out:
+            copy.start()
+
+    def add_pair(self, start=0, stop=None):
+        for i in range(len(self.owners))[start:stop]:
+            self.pair_out[i].wait_recv()
+            rows = rows_at(self.owners[i] * self.rows, self.rows)
+            self.pair[rows, :] = self.pair[rows, :] + self.grad[rows, self.mine]
+            self.other_out[i].start()
+
+    def sent_pair(self):
+        for copy in self.pair_out:
+            copy.wait_send()
+
+    def add_other(self, start=0, stop=None):
+        where = self.where
+        for i in range(len(self.owners))[start:stop]:
+            self.other_in[i].wait_recv()
+            owner = self.owners[i]
+            mine = rows_at(owner * self.rows + where.plane * self.ring_rows, self.shared)
+            theirs = rows_at(owner * self.shared, self.shared)
+            self.pair[mine, :] = self.pair[mine, :] + self.other[theirs, :]
+            if i == 0:
+                self.ring_send(1)
+
+    def ring_send(self, step):
+        for direction in range(2):
+            self.ring_out[direction, step].start()
+
+    def ring_step(self, step):
+        far = self.where.far
+        for direction in range(2):
+            start, size = self.span(direction, step)
+            self.ring_in[direction, step].wait_recv()
+            if step < far:
+                rows = self.ring_rows_of(self.target(direction, far - step), start, size)
+                came = self.passing[direction, step - 1, pl.ds(start, size)]
+                self.pair[rows, :] = self.pair[rows, :] + came
+        if step < far:
+            self.ring_send(step + 1)
+            return
+        total = self.pair[self.own, :].astype(jnp.float32)
+        total = total + self.passing[0, step - 1].astype(jnp.float32)
+        total = total + self.passing[1, step - 1].astype(jnp.float32)
+        self.pair[self.own, :] = total.astype(jnp.bfloat16)
+        self.final_out.start()
+
+    def finish(self):
+        where = self.where
+        self.final_in.wait_recv()
+        columns = self.mine
+        plane, shared, ring_rows = where.plane, self.shared, self.ring_rows
+        both = self.rows - 2 * shared
+        base = where.fsdp * self.rows + plane * shared
+        f32 = jnp.float32
+        if both:
+            mine = self.pair[rows_at(base + (1 - plane) * shared, both), :].astype(f32)
+            theirs = self.final[rows_at(plane * shared, both), :].astype(f32)
+            self.out[pl.ds(shared, both), columns] = mine + theirs
+        mine = self.pair[rows_at(base + plane * (ring_rows - shared), shared), :]
+        self.out[rows_at(plane * ring_rows, shared), columns] = mine.astype(f32)
+        theirs = self.final[rows_at((1 - plane) * (ring_rows - shared), shared), :]
+        self.out[rows_at((1 - plane) * ring_rows, shared), columns] = theirs.astype(f32)
+        self.out_out.start()
+
+    def close(self):
+        self.out_in.wait_recv()
+        for copy in self.other_out + list(self.ring_out.values()) + [self.final_out, self.out_out]:
+            copy.wait_send()
+
+
+SEG_ROWS = (1, 1, 3, 2, 1, 1, 1, 4, 1)
+(G1, B1, QB, FR, OB, G2, B2, F1B, F2B) = range(9)
+MLP = 3072
+
+
+def offsets():
+    starts, total = [], 0
+    for m in SEG_ROWS:
+        starts.append(total)
+        total += m
+    return starts, total
+
+
+def unpack_small(slots, vec, count, seg):
+    lane = lax.broadcasted_iota(jnp.int32, (1, 128), 1)
+    starts, _ = offsets()
+    for first, m in zip(starts, SEG_ROWS):
+        pieces = [jnp.zeros((1, 128), jnp.float32) for _ in range(m * count * seg // 128)]
+        for f in range(count):
+            for i in range(m):
+                at = (m * f + i) * seg
+                v, s = at // 128, at % 128
+                row = slots[f, first + i : first + i + 1, :]
+                if s:
+                    row = pltpu.roll(row, s, 1)
+                pieces[v] = pieces[v] + jnp.where(lane >= s, row, 0.0)
+                if s + seg > 128:
+                    pieces[v + 1] = pieces[v + 1] + jnp.where(lane < s + seg - 128, row, 0.0)
+        for v, piece in enumerate(pieces):
+            at = first * count * seg + 128 * v
+            vec[:, at : at + 128] = piece
+
+
+def part_of(vec, which, start=0, size=None):
+    starts, _ = offsets()
+    base = starts[which] * D
+    size = SEG_ROWS[which] * D if size is None else size
+    return vec[:, base + start : base + start + size]
+
+
+def half_swap(t):
+    width = t.shape[-1]
+    lane = lax.broadcasted_iota(jnp.int32, t.shape, 1)
+    return jnp.where(lax.rem(lane, HD) < HD // 2, pltpu.roll(t, width - HD // 2, 1), pltpu.roll(t, HD // 2, 1))
+
+
+def columns_down(ref, i):
+    return jnp.broadcast_to(ref[i : i + 1, :], (128, 128)).T
+
+
+def rope_tables(vec, col, row, cosine, sine, tables):
+    step = lax.broadcasted_iota(jnp.int32, (32, D), 0).astype(jnp.float32)
+    stacks = []
+    for at in (0, D):
+        angle = step * part_of(vec, FR, at, D)
+        for table in (jnp.cos(angle), jnp.sin(angle)):
+            high = table.astype(jnp.bfloat16)
+            rest = table - high.astype(jnp.float32)
+            middle = rest.astype(jnp.bfloat16)
+            last = (rest - middle.astype(jnp.float32)).astype(jnp.bfloat16)
+            stacks.append(jnp.concatenate([high, middle, last, jnp.zeros_like(high)], axis=0))
+            tables[len(stacks) - 1] = stacks[-1]
+    lane = lax.broadcasted_iota(jnp.int32, (128, 128), 1)
+    slot = jnp.where(lane < 96, lax.rem(lane, 32), -1).astype(jnp.float32)
+    wide = lax.broadcasted_iota(jnp.int32, (128, D), 1)
+    sign = jnp.where(lax.rem(wide, HD) < HD // 2, -1.0, 1.0)
+    for i in range(col.shape[0]):
+        at = pl.ds(128 * i, 128)
+        pick_col = jnp.where(columns_down(col, i) == slot, 1.0, 0.0).astype(jnp.bfloat16)
+        pick_row = jnp.where(columns_down(row, i) == slot, 1.0, 0.0).astype(jnp.bfloat16)
+        look = lambda pick, stack: jnp.dot(pick, stack, preferred_element_type=jnp.float32)
+        cc, cs = look(pick_col, stacks[0]), look(pick_col, stacks[1])
+        rc, rs = look(pick_row, stacks[2]), look(pick_row, stacks[3])
+        cosine[at, :] = cc * rc - cs * rs
+        sine[at, :] = (cs * rc + cc * rs) * sign
+
+
+def image_bias(image, bias):
+    for i in range(image.shape[0]):
+        mine = columns_down(image, i)
+        for j in range(image.shape[0]):
+            same = mine == image[j : j + 1, :]
+            bias[128 * i : 128 * i + 128, 128 * j : 128 * j + 128] = jnp.where(same, 0.0, MASKED)
+
+
+def turn(source, target, start=0):
+    def body(j):
+        target[pl.ds(pl.multiple_of(start + 128 * j, 128), 128), :] = source[:, tile_at(j, 128)].T
+
+    loop(source.shape[1] // 128, body)
+
+
+def statistics(values):
+    centre = values - jnp.mean(values, axis=-1, keepdims=True)
+    spread = jnp.mean(centre * centre, axis=-1, keepdims=True)
+    inverse = lax.rsqrt(spread + EPSILON)
+    return centre * inverse, inverse
+
+
+def loop(count, body):
+    def run(i, carry):
+        body(i)
+        return carry
+
+    lax.fori_loop(0, count, run, 0)
+
+
+def tile_at(i, size):
+    return pl.ds(pl.multiple_of(i * size, size), size)
+
+
+def matmul(left, right):
+    return jnp.dot(left, right, preferred_element_type=jnp.float32)
+
+
+def matmul_nt(left, right):
+    return lax.dot_general(left, right, (((1,), (1,)), ((), ())), preferred_element_type=jnp.float32)
+
+
+def project(normed_low, weights, vec, cosine, sine, outs):
+    tile = 256
+    per = D // tile
+    for which, out in enumerate(outs):
+        def body(j, which=which, out=out):
+            cols = tile_at(j, tile)
+            wide = pl.ds(pl.multiple_of(which * D + j * tile, tile), tile)
+            starts, _ = offsets()
+            shift = vec[:, pl.ds(pl.multiple_of(starts[QB] * D + which * D + j * tile, tile), tile)]
+            t = matmul(normed_low[...], weights[:, wide]) + shift
+            if which < 2:
+                t = t * cosine[:, cols] + half_swap(t) * sine[:, cols]
+            if which == 0:
+                t = t * HD**-0.5
+            out[:, cols] = t.astype(jnp.bfloat16)
+
+        loop(per, body)
+
+
+def attend(pair, query, key, value, bias, mixed, lse, block):
+    lane_all = lax.broadcasted_iota(jnp.int32, (1, 128), 1)
+    cols = tile_at(pair, 128)
+    lane = lax.broadcasted_iota(jnp.int32, (1, 128), 1)
+    first = lane < HD
+    k2, v2 = key[:, cols], value[:, cols]
+    zero = jnp.zeros((), jnp.bfloat16)
+    for start in range(0, query.shape[0], block):
+        rows = pl.ds(start, block)
+        q2 = query[rows, cols]
+        total, sums, tops = None, [], []
+        for keep in (first, ~first):
+            s = matmul_nt(jnp.where(keep, q2, zero), k2) + bias[rows, :]
+            top = jnp.max(s, axis=-1, keepdims=True)
+            p = jnp.exp(s - top)
+            sums.append(jnp.sum(p, axis=-1, keepdims=True))
+            tops.append(top)
+            o = matmul(p.astype(jnp.bfloat16), jnp.where(keep, v2, zero))
+            total = o if total is None else total + o
+        mixed[rows, cols] = (total / jnp.where(first, sums[0], sums[1])).astype(jnp.bfloat16)
+        kept = lse[rows, :]
+        for i in range(2):
+            kept = jnp.where(lane_all == 2 * pair + i, tops[i] + jnp.log(sums[i]), kept)
+        lse[rows, :] = kept
+
+
+def norm_rows(source, normed_low, vec, gain, shift, block=128):
+    def body(i):
+        rows = tile_at(i, block)
+        unit, _ = statistics(source[rows, :].astype(jnp.float32))
+        normed_low[rows, :] = (unit * part_of(vec, gain) + part_of(vec, shift)).astype(jnp.bfloat16)
+
+    loop(source.shape[0] // block, body)
+
+
+def mix_out(x, mixed, weights, vec, middle):
+    starts, _ = offsets()
+
+    def body(j):
+        cols = tile_at(j, 256)
+        shift = vec[:, pl.ds(pl.multiple_of(starts[OB] * D + j * 256, 256), 256)]
+        middle[:, cols] = x[:, cols].astype(jnp.float32) + matmul(mixed[...], weights[:, cols]) + shift
+
+    loop(D // 256, body)
+
+
+def hidden_tile(j, normed_low, weights, vec, active, active_t, slope):
+    starts, _ = offsets()
+    cols = tile_at(j, 256)
+    shift = vec[:, pl.ds(pl.multiple_of(starts[F1B] * D + j * 256, 256), 256)]
+    h = matmul(normed_low[...], weights[:, cols]) + shift
+    c = (2.0 / math.pi) ** 0.5
+    square = h * h
+    t = jnp.tanh(c * h * (1.0 + 0.044715 * square))
+    low = (0.5 * h * (1.0 + t)).astype(jnp.bfloat16)
+    active[:, cols] = low
+    active_t[cols, :] = low.T
+    slope[:, cols] = (
+        0.5 * (1.0 + t) + 0.5 * h * (1.0 - t * t) * (c * (1.0 + 3 * 0.044715 * square))
+    ).astype(jnp.bfloat16)
+
+
+def result_tile(j, middle, active, weights, vec, output):
+    starts, _ = offsets()
+    cols = tile_at(j, 256)
+    shift = vec[:, pl.ds(pl.multiple_of(starts[F2B] * D + j * 256, 256), 256)]
+    output[:, cols] = (middle[:, cols] + matmul(active[...], weights[:, cols]) + shift).astype(jnp.bfloat16)
+
+
+def forward_kernel(count, seg, shares, *refs):
+    (x, image, row, col, small, qkv_s, out_s, fc1_s, fc2_s) = refs[:9]
+    (output, vec_o, tables_o, turned_o, q_o, k_o, v_o, lse_o, middle_o, act_t_o, slope_o,
+     qkv_o, out_o, fc1_o, fc2_o) = refs[9:24]
+    (slots, vec, tables, turned, q, k, v, lse_t, middle, act_t, slope, qkv_w, out_w, fc1_w, fc2_w,
+     cosine, sine, bias, lse, act, low,
+     send, recv, small_send, small_recv, local, saved) = refs[24:]
+    n1 = mixed = n2 = low
+    where = Place(count)
+    peers = [(lax.rem(where.fsdp + i, count), where.dp) for i in range(1, count)]
+    where.greet(peers)
+    sems = Sems(send, recv)
+    flows = [
+        Gather(where, sems, s, w, shared, local.at[i])
+        for i, (s, w, shared) in enumerate(
+            zip((qkv_s, out_s, fc1_s, fc2_s), (qkv_w, out_w, fc1_w, fc2_w), shares)
+        )
+    ]
+    qkv_f, out_f, fc1_f, fc2_f = flows
+    far = where.far
+    small_copies = [
+        remote(small, slots.at[where.fsdp], (small_send.at[i], small_recv.at[i]), peers[i])
+        for i in range(count - 1)
+    ]
+    for copy in small_copies:
+        copy.start()
+    qkv_f.start()
+    out_f.start()
+    slots[where.fsdp] = small[...]
+    saves = []
+
+    def save(source, target):
+        copy = pltpu.make_async_copy(source, target, saved.at[len(saves)])
+        copy.start()
+        saves.append(copy)
+
+    image_bias(image, bias)
+    for i in range(1, count):
+        came = slots.at[lax.rem(where.fsdp + count - i, count)]
+        remote(came, came, (small_send.at[i - 1], small_recv.at[i - 1]), peers[i - 1]).wait_recv()
+    unpack_small(slots, vec, count, seg)
+    save(vec, vec_o)
+    norm_rows(x, n1, vec, G1, B1)
+    turn(n1, turned)
+    qkv_f.tick(1)
+    fc1_f.start()
+    out_f.tick(1)
+    rope_tables(vec, col, row, cosine, sine, tables)
+    save(tables, tables_o)
+    lse[...] = jnp.zeros_like(lse)
+    for step in range(2, far + 2):
+        qkv_f.tick(step)
+        out_f.tick(step)
+        if step == 3:
+            fc2_f.start()
+            fc1_f.tick(1)
+    qkv_f.finish()
+    project(n1, qkv_w, vec, cosine, sine, (q, k, v))
+    out_f.finish()
+    save(qkv_w, qkv_o)
+    save(out_w, out_o)
+    save(q, q_o)
+    save(k, k_o)
+    save(v, v_o)
+
+    ticks = [(fc2_f, 1), (fc1_f, 2), (fc2_f, 2), (fc1_f, 3), (fc2_f, 3), (fc1_f, 4), (fc2_f, 4), (fc1_f, 5)]
+    ticks = ticks if far == 4 else []
+
+    def pair_body(j):
+        attend(j, q, k, v, bias, mixed, lse, 320)
+        for i, (flow, step) in enumerate(ticks):
+            @pl.when(j == min(i // 2 + 1, 5))
+            def _(flow=flow, step=step):
+                flow.tick(step)
+
+    loop(H // 2, pair_body)
+    lse_t[...] = lse[...].T
+    save(lse_t, lse_o)
+    turn(mixed, turned, D)
+    mix_out(x, mixed, out_w, vec, middle)
+    save(middle, middle_o)
+    norm_rows(middle, n2, vec, G2, B2)
+    turn(n2, turned, 2 * D)
+    save(turned, turned_o)
+    fc2_f.tick(far + 1)
+    fc1_f.finish()
+    loop(MLP // 256, lambda j: hidden_tile(j, n2, fc1_w, vec, act, act_t, slope))
+    save(act_t, act_t_o)
+    save(slope, slope_o)
+    save(fc1_w, fc1_o)
+    fc2_f.finish()
+    save(fc2_w, fc2_o)
+    loop(D // 256, lambda j: result_tile(j, middle, act, fc2_w, vec, output))
+    for flow in flows:
+        flow.drain()
+    for copy in small_copies:
+        copy.wait_send()
+    for copy in saves:
+        copy.wait()
+
+
+def forward(x, image, row, col, small, weights, count):
+    bf16, f32 = jnp.bfloat16, jnp.float32
+    tokens = x.shape[0]
+    seg = D // count
+    shares = tuple(w.shape[0] // 3 for w in weights)
+    wide = lambda kind, width=D: ((tokens, width), kind)
+    total = offsets()[1] * D
+    full = [((w.shape[0] * count, w.shape[1]), bf16) for w in weights]
+    kept = [
+        ((1, total), f32), ((4, 128, D), bf16), ((3 * D, tokens), bf16), wide(bf16), wide(bf16), wide(bf16),
+        ((128, tokens), f32), wide(f32), ((MLP, tokens), bf16), wide(bf16, MLP),
+    ] + full
+    copies = 4 * 8 * (count // 2)
+    any_spec = pl.BlockSpec(memory_space=pl.ANY)
+    vmem_spec = pl.BlockSpec(memory_space=pltpu.VMEM)
+    scratch = kept + [
+        wide(f32), wide(f32), ((tokens, tokens), f32), wide(f32, 128), wide(bf16, MLP), wide(bf16),
+    ]
+    return pl.pallas_call(
+        partial(forward_kernel, count, seg, shares),
+        out_shape=[jax.ShapeDtypeStruct((tokens, D), bf16)] + [jax.ShapeDtypeStruct(*s) for s in kept],
+        in_specs=[vmem_spec] * 9,
+        out_specs=[vmem_spec] + [any_spec] * len(kept),
+        scratch_shapes=[pltpu.VMEM((count,) + small.shape, f32)]
+        + [pltpu.VMEM(*s) for s in scratch]
+        + [
+            pltpu.SemaphoreType.DMA((copies,)),
+            pltpu.SemaphoreType.DMA((copies,)),
+            pltpu.SemaphoreType.DMA((count - 1,)),
+            pltpu.SemaphoreType.DMA((count - 1,)),
+            pltpu.SemaphoreType.DMA((4,)),
+            pltpu.SemaphoreType.DMA((len(kept),)),
+        ],
+        compiler_params=pltpu.CompilerParams(
+            collective_id=0, has_side_effects=True, vmem_limit_bytes=67043328
+        ),
+        name="forward",
+    )(x, image, row, col, small, *weights)
+
+
+def unit_and_inverse(source, rows):
+    return statistics(source[rows, :].astype(jnp.float32))
+
+
+def attend_back(pair, query, key, value, lse_t, bias, tables, pick_col, pick_row, colb, rowb, given, grads, sums, blocks):
+    cols = tile_at(pair, 128)
+    f32, bf16 = jnp.float32, jnp.bfloat16
+    tokens = query.shape[0]
+    lane = lax.broadcasted_iota(jnp.int32, (1, 128), 1)
+    first = lane < HD
+    zero = jnp.zeros((), bf16)
+    q2, k2, v2, g2 = query[:, cols], key[:, cols], value[:, cols], given[:, cols]
+    k2_t = k2.T
+    grad_key = jnp.zeros((tokens, 128), f32)
+    grad_value = jnp.zeros((tokens, 128), f32)
+    turned = []
+    for start, size in blocks:
+        rows = slice(start, start + size)
+        halves = []
+        for i, keep in enumerate((first, ~first)):
+            q1 = jnp.where(keep, q2[rows], zero)
+            g1 = jnp.where(keep, g2[rows], zero)
+            s = matmul_nt(k2, q1) + bias[:, rows]
+            heads = lse_t[0:16, rows]
+            head = lax.broadcasted_iota(jnp.int32, heads.shape, 0)
+            p = jnp.exp(s - jnp.sum(jnp.where(head == 2 * pair + i, heads, 0.0), axis=0, keepdims=True))
+            gp = matmul_nt(v2, g1)
+            ds = p * (gp - jnp.sum(p * gp, axis=0, keepdims=True))
+            ds = ds.astype(bf16)
+            grad_value = grad_value + matmul(p.astype(bf16), g1)
+            grad_key = grad_key + matmul(ds, q1)
+            halves.append(matmul(k2_t[HD * i : HD * i + HD], ds))
+        turned.append(jnp.concatenate(halves, axis=0).T)
+    grad_query = jnp.concatenate(turned, axis=0) * HD**-0.5
+    look = lambda pick, i: jnp.dot(pick[...], tables[i, :, cols], preferred_element_type=f32)
+    cc, cs, rc, rs = look(pick_col, 0), look(pick_col, 1), look(pick_row, 2), look(pick_row, 3)
+    sign = jnp.where(lax.rem(lane, HD) < HD // 2, -1.0, 1.0)
+    cosine, sine = cc * rc - cs * rs, (cs * rc + cc * rs) * sign
+    turn_sum = half_swap(q2.astype(f32)) * (grad_query * HD**0.5) + half_swap(k2.astype(f32)) * grad_key
+    starts, _ = offsets()
+    for i, where_at in enumerate((colb, rowb)):
+        at = pl.ds(pl.multiple_of((starts[FR] + i) * D + 128 * pair, 128), 128)
+        sums[:, at] = jnp.sum(turn_sum * where_at[...], axis=0, keepdims=True) * sign
+    finals = (
+        grad_query * cosine - half_swap(grad_query) * sine,
+        grad_key * cosine - half_swap(grad_key) * sine,
+        grad_value,
+    )
+    for i, final in enumerate(finals):
+        low = final.astype(bf16)
+        at = pl.ds(pl.multiple_of(i * D + 128 * pair, 128), 128)
+        grads[:, at] = low
+        at = pl.ds(pl.multiple_of((starts[QB] + i) * D + 128 * pair, 128), 128)
+        sums[:, at] = jnp.sum(low.astype(f32), axis=0, keepdims=True)
+
+
+def norm_back(source, grad, onward, gain, vec, sums, which_gain, which_shift, emit, block=128):
+    starts, _ = offsets()
+    gain_at = slice(starts[which_gain] * D, starts[which_gain] * D + D)
+    shift_at = slice(starts[which_shift] * D, starts[which_shift] * D + D)
+    sums[:, gain_at] = jnp.zeros((1, D), jnp.float32)
+    sums[:, shift_at] = jnp.zeros((1, D), jnp.float32)
+
+    def body(i):
+        rows = tile_at(i, block)
+        unit, inverse = statistics(source[rows, :].astype(jnp.float32))
+        g = grad[rows, :]
+        sums[:, gain_at] += jnp.sum(g * unit, axis=0, keepdims=True)
+        sums[:, shift_at] += jnp.sum(g, axis=0, keepdims=True)
+        e = g * part_of(vec, gain)
+        mean = jnp.mean(e, axis=-1, keepdims=True)
+        along = jnp.mean(e * unit, axis=-1, keepdims=True)
+        emit(rows, onward[rows, :].astype(jnp.float32) + inverse * (e - mean - unit * along))
+
+    loop(source.shape[0] // block, body)
+
+
+def pack_sums(sums, slots, count, seg):
+    lane = lax.broadcasted_iota(jnp.int32, (1, 128), 1)
+    starts, _ = offsets()
+    slots[...] = jnp.zeros_like(slots)
+    for first, m in zip(starts, SEG_ROWS):
+        for f in range(count):
+            for i in range(m):
+                at = first * count * seg + (m * f + i) * seg
+                v, s = at // 128, at % 128
+                row = sums[:, 128 * v : 128 * v + 128]
+                if s:
+                    row = pltpu.roll(row, 128 - s, 1)
+                if s + seg > 128:
+                    more = pltpu.roll(sums[:, 128 * v + 128 : 128 * v + 256], 128 - s, 1)
+                    row = jnp.where(lane < 128 - s, row, more)
+                slots[f, first + i : first + i + 1, :] = jnp.where(lane < seg, row, 0.0)
+
+
+def backward_kernel(count, seg, shared, wide_shared, *refs):
+    (x, grad_out, image, row, col, vec_h, tables_h, turned_h, q_h, k_h, v_h, lse_h, middle_h, act_t_h, slope_h,
+     qkv_h, out_h, fc1_h, fc2_h) = refs[:19]
+    (grad_x, small_out, grad_qkv, grad_out_w, grad_fc1, grad_fc2) = refs[19:25]
+    (vec, tables, q, k, v, lse_t, middle, act_t, slope, out_w, fc1_w, fc2_w,
+     bias, pick_col, pick_row, colb, rowb, wide, low, big, sums, slots, slots_twin, slots_across, slots_in) = refs[25:50]
+    outs = refs[50:57]
+    bufs = refs[57:93]
+    send, recv, small_send, small_recv, loaded = refs[93:]
+    f32, bf16 = jnp.float32, jnp.bfloat16
+    where = Place(count)
+    far = where.far
+    starts, _ = offsets()
+
+    loads = {}
+
+    def load(name, source, target):
+        copy = pltpu.make_async_copy(source, target, loaded.at[len(loads)])
+        copy.start()
+        loads[name] = copy
+
+    load("act", act_t_h, act_t)
+    load("fc2", fc2_h, fc2_w)
+    load("slope", slope_h, slope)
+    load("fc1", fc1_h, fc1_w)
+    for name, source, target in (
+        ("vec", vec_h, vec), ("middle", middle_h, middle), ("out", out_h, out_w), ("q", q_h, q), ("k", k_h, k),
+        ("v", v_h, v), ("lse", lse_h, lse_t), ("tables", tables_h, tables),
+    ):
+        load(name, source, target)
+    peers = [(lax.rem(where.fsdp + i, count), where.dp) for i in range(1, count)]
+    where.greet(peers)
+    sems = Sems(send, recv)
+    fc2 = Reduce(where, sems, big, grad_fc2, wide_shared, bufs[:4])
+    parts = [
+        Reduce(
+            where, sems, big.at[pl.ds(D * (i % 4), D)], grad_out_w if i == 4 else outs[i - (i > 4)],
+            shared, bufs[4 + 4 * i : 8 + 4 * i],
+        )
+        for i in range(8)
+    ]
+
+    loads["act"].wait()
+    loop(8, lambda i: store_tile(big, i, 384, act_t, grad_out))
+    fc2.start()
+    at = starts[F2B] * D
+    sums[:, at : at + D] = jnp.sum(grad_out[...].astype(f32), axis=0, keepdims=True)
+    loads["fc2"].wait()
+    loads["slope"].wait()
+    load("turned", turned_h, act_t.at[pl.ds(0, 3 * D)])
+    normed_one, mixed_t, normed_two = (act_t.at[pl.ds(D * i, D)] for i in range(3))
+
+    def hidden(j):
+        cols = tile_at(j, 256)
+        g = matmul_nt(grad_out[...], fc2_w[cols, :]) * slope[:, cols].astype(f32)
+        g = g.astype(bf16)
+        slope[:, cols] = g
+        at = pl.ds(pl.multiple_of(starts[F1B] * D + 256 * j, 256), 256)
+        sums[:, at] = jnp.sum(g.astype(f32), axis=0, keepdims=True)
+
+    loop(MLP // 256, hidden)
+    fc2.add_pair()
+    fc2.sent_pair()
+    loads["turned"].wait()
+    for i in range(4):
+        grad_part = slope.at[:, pl.ds(D * i, D)]
+        loop(2, lambda j: store_tile(big.at[pl.ds(D * i, D)], j, 384, normed_two, grad_part))
+        parts[i].start()
+        if i:
+            parts[i - 1].add_pair()
+        if i == 1:
+            fc2.add_other()
+        if i == 3:
+            fc2.ring_step(1)
+    loads["fc1"].wait()
+
+    def normed_grad(j):
+        cols = tile_at(j, 256)
+        wide[:, cols] = matmul_nt(slope[...], fc1_w[cols, :])
+
+    normed_grad(0)
+    parts[3].add_pair()
+    parts[0].add_other()
+    normed_grad(1)
+    parts[1].add_other()
+    fc2.ring_step(2)
+    parts[0].ring_step(1)
+    normed_grad(2)
+    for i in range(4):
+        parts[i].sent_pair()
+    load("qkv", qkv_h, big_rows(fc1_w))
+    loads["vec"].wait()
+    loads["middle"].wait()
+    parts[2].add_other()
+    parts[1].ring_step(1)
+
+    at = starts[OB] * D
+    sums[:, at : at + D] = jnp.zeros((1, D), f32)
+
+    def keep_middle(rows, total):
+        wide[rows, :] = total
+        total = total.astype(bf16)
+        low[rows, :] = total
+        sums[:, at : at + D] += jnp.sum(total.astype(f32), axis=0, keepdims=True)
+
+    norm_back(middle, wide, grad_out, G2, vec, sums, G2, B2, keep_middle)
+    parts[3].add_other()
+    fc2.ring_step(3)
+    parts[0].ring_step(2)
+    parts[2].ring_step(1)
+    loop(2, lambda j: store_tile(big.at[pl.ds(0, D)], j, 384, mixed_t, low))
+    parts[4].start()
+    loads["out"].wait()
+    mixed_grad = slope.at[:, pl.ds(3 * D, D)]
+
+    def mix_back(j):
+        cols = tile_at(j, 256)
+        mixed_grad[:, cols] = matmul_nt(low[...], out_w[cols, :]).astype(bf16)
+
+    loop(D // 256, mix_back)
+    parts[4].add_pair()
+
+    image_bias(image, bias)
+    lane = lax.broadcasted_iota(jnp.int32, (128, 128), 1)
+    slot = jnp.where(lane < 96, lax.rem(lane, 32), -1).astype(f32)
+    for i in range(col.shape[0]):
+        rows = slice(128 * i, 128 * i + 128)
+        for source, kept, pick in ((col, colb, pick_col), (row, rowb, pick_row)):
+            down = columns_down(source, i)
+            kept[rows, :] = down
+            pick[rows, :] = jnp.where(down == slot, 1.0, 0.0).astype(bf16)
+    for name in ("q", "k", "v", "lse", "tables"):
+        loads[name].wait()
+
+    turns = {
+        0: [lambda: parts[3].ring_step(1), lambda: fc2.ring_step(4), lambda: parts[0].ring_step(3),
+            lambda: parts[1].ring_step(2), lambda: parts[4].add_other()],
+        1: [lambda: parts[2].ring_step(2), lambda: parts[0].ring_step(4), lambda: parts[3].ring_step(2),
+            lambda: parts[1].ring_step(3), lambda: parts[4].ring_step(1)],
+        2: [lambda: fc2.finish(), lambda: parts[2].ring_step(3), lambda: parts[1].ring_step(4),
+            lambda: parts[3].ring_step(3), lambda: parts[4].ring_step(2), lambda: parts[5].add_pair()],
+        3: [lambda: parts[0].finish(), lambda: parts[2].ring_step(4), lambda: parts[3].ring_step(4),
+            lambda: parts[4].ring_step(3), lambda: parts[5].add_other()],
+        4: [lambda: parts[1].finish(), lambda: parts[4].ring_step(4), lambda: parts[5].ring_step(1),
+            lambda: parts[6].add_pair()],
+        5: [lambda: parts[2].finish(), lambda: parts[5].ring_step(2), lambda: parts[6].add_other()],
+    }
+    tokens = q.shape[0]
+    blocks = [(i, min(256, tokens - i)) for i in range(0, tokens, 256)]
+
+    def pair_body(j):
+        attend_back(
+            j, q, k, v, lse_t, bias, tables, pick_col, pick_row, colb, rowb, mixed_grad, slope, sums, blocks
+        )
+        for i, steps in turns.items():
+            @pl.when(j == i)
+            def _(i=i, steps=steps):
+                if i % 2:
+                    project_back(parts[5 + i // 2].grad, normed_one, slope, i // 2)
+                    parts[5 + i // 2].start()
+                for step in steps:
+                    step()
+
+    loop(H // 2, pair_body)
+    loads["qkv"].wait()
+    qkv_w = big_rows(fc1_w)
+    parts[7].add_pair()
+    parts[5].ring_step(3)
+    parts[6].ring_step(1)
+
+    def normed_one_grad(j):
+        cols = tile_at(j, 256)
+        middle[:, cols] = matmul_nt(slope[:, pl.ds(0, 3 * D)], qkv_w[cols, :])
+
+    normed_one_grad(0)
+    parts[7].add_other()
+    parts[5].ring_step(4)
+    parts[6].ring_step(2)
+    normed_one_grad(1)
+    parts[7].ring_step(1)
+    parts[6].ring_step(3)
+    parts[3].finish()
+    normed_one_grad(2)
+    parts[7].ring_step(2)
+    parts[6].ring_step(4)
+    parts[4].finish()
+
+    def keep_x(rows, total):
+        grad_x[rows, :] = total.astype(bf16)
+
+    norm_back(x, middle, wide, G1, vec, sums, G1, B1, keep_x)
+    parts[7].ring_step(3)
+    pack_sums(sums, slots, count, seg)
+    take = lambda i: (small_send.at[i], small_recv.at[i])
+    to_twin = remote(slots, slots_twin, take(0), where.twin)
+    to_twin.start()
+    parts[5].finish()
+    parts[7].ring_step(4)
+    to_twin.wait()
+    slots[...] = slots[...] + slots_twin[...]
+    to_across = remote(slots, slots_across, take(1), where.across)
+    to_across.start()
+    parts[6].finish()
+    to_across.wait()
+    slots[...] = slots[...] + slots_across[...]
+    slots_in[where.fsdp] = slots[where.fsdp]
+    given = [
+        remote(slots.at[peer[0]], slots_in.at[where.fsdp], take(2 + i), peer) for i, peer in enumerate(peers)
+    ]
+    for copy in given:
+        copy.start()
+    parts[7].finish()
+    for i in range(1, count):
+        came = slots_in.at[lax.rem(where.fsdp + count - i, count)]
+        remote(came, came, take(1 + i), peers[i - 1]).wait_recv()
+    total = slots_in[0]
+    for i in range(1, count):
+        total = total + slots_in[i]
+    small_out[...] = total
+    for copy in given:
+        copy.wait_send()
+    for i in range(4, 8):
+        parts[i].sent_pair()
+    fc2.close()
+    for part in parts:
+        part.close()
+    for i in range(4):
+        grad_fc1[:, pl.ds(D * i, D)] = outs[i][...]
+    for m in range(3):
+        for i in range(3):
+            grad_qkv[:, pl.ds(i * D + 256 * m, 256)] = outs[4 + m][:, pl.ds(256 * i, 256)]
+
+
+def store_tile(target, i, size, left, right):
+    rows = tile_at(i, size)
+    target[rows, :] = matmul(left[rows, :], right[...]).astype(jnp.bfloat16)
+
+
+def big_rows(ref):
+    return ref.at[:, pl.ds(0, 3 * D)]
+
+
+def project_back(target, normed, grads, m):
+    for i in range(3):
+        target[:, pl.ds(256 * i, 256)] = matmul(normed[...], grads[:, pl.ds(i * D + 256 * m, 256)]).astype(jnp.bfloat16)
+
+
+def backward(x, grad_out, image, row, col, kept, count):
+    bf16, f32 = jnp.bfloat16, jnp.float32
+    tokens = x.shape[0]
+    seg = D // count
+    shared, wide_shared = seg // 96 * 16, seg
+    (vec, tables, turned, q, k, v, lse, middle, act_t, slope, qkv, out, fc1, fc2) = kept
+    like = lambda a: pltpu.VMEM(a.shape, a.dtype)
+    side = pltpu.VMEM((tokens, 128), f32)
+    pick = pltpu.VMEM((tokens, 128), bf16)
+    slots = pltpu.VMEM((count, 16, 128), f32)
+    part = pltpu.VMEM((seg, D), f32)
+    flows = Reduce.shapes(MLP // count, D, count, wide_shared)
+    for _ in range(8):
+        flows = flows + Reduce.shapes(seg, D, count, shared)
+    copies = 9 * Reduce.copies(count)
+    any_spec = pl.BlockSpec(memory_space=pl.ANY)
+    vmem_spec = pl.BlockSpec(memory_space=pltpu.VMEM)
+    dma = pltpu.SemaphoreType.DMA
+    return pl.pallas_call(
+        partial(backward_kernel, count, seg, shared, wide_shared),
+        out_shape=[
+            jax.ShapeDtypeStruct((tokens, D), bf16),
+            jax.ShapeDtypeStruct((16, 128), f32),
+            jax.ShapeDtypeStruct((seg, 3 * D), f32),
+            jax.ShapeDtypeStruct((seg, D), f32),
+            jax.ShapeDtypeStruct((seg, MLP), f32),
+            jax.ShapeDtypeStruct((MLP // count, D), f32),
+        ],
+        in_specs=[vmem_spec] * 5 + [any_spec] * len(kept),
+        out_specs=[vmem_spec] * 6,
+        scratch_shapes=[like(a) for a in (vec, tables, q, k, v, lse, middle, act_t, slope, out, fc1, fc2)]
+        + [
+            pltpu.VMEM((tokens, tokens), f32), pick, pick, side, side,
+            pltpu.VMEM((tokens, D), f32), pltpu.VMEM((tokens, D), bf16), pltpu.VMEM((MLP, D), bf16),
+            pltpu.VMEM(vec.shape, f32), slots, slots, slots, slots,
+        ]
+        + [part] * 7
+        + flows
+        + [dma((copies,)), dma((copies,)), dma((count + 1,)), dma((count + 1,)), dma((len(kept),))],
+        compiler_params=pltpu.CompilerParams(
+            collective_id=1, has_side_effects=True, vmem_limit_bytes=67043328
+        ),
+        name="backward",
+    )(x, grad_out, image, row, col, *kept)
+
+
+def pack_small(parts, count):
+    seg = D // count
+    rows = []
+    for i, part in enumerate(parts):
+        if i == FR:
+            part = jnp.broadcast_to(part.reshape(-1, 1, HD // 2), (seg // (HD // 2), 2, HD // 2))
+        rows.append(part.reshape(-1, seg))
+    rows = jnp.concatenate(rows, axis=0).astype(jnp.float32)
+    return jnp.pad(rows, ((0, -rows.shape[0] % 8), (0, 128 - seg)))
 
 
 def normed(values, scales, shifts):
@@ -304,6 +1361,64 @@
     )
 
 
+def fast_body(
+    layer_in,
+    ln1_gain,
+    ln1_bias,
+    qkv_weight,
+    qkv_bias,
+    rope_freqs,
+    out_weight,
+    out_bias,
+    ln2_gain,
+    ln2_bias,
+    fc1_weight,
+    fc1_bias,
+    fc2_weight,
+    fc2_bias,
+    image_of,
+    patch_row,
+    patch_col,
+    grad_out,
+):
+    count = lax.axis_size("fsdp")
+    seg = D // count
+    parts = (ln1_gain, ln1_bias, qkv_bias, rope_freqs, out_bias, ln2_gain, ln2_bias, fc1_bias, fc2_bias)
+    small = pack_small(parts, count)
+    image, row, col = (a.reshape(-1, 128).astype(jnp.float32) for a in (image_of, patch_row, patch_col))
+    output, *kept = forward(
+        layer_in, image, row, col, small, (qkv_weight, out_weight, fc1_weight, fc2_weight), count
+    )
+    grad_x, sums, grad_qkv, grad_out_w, grad_fc1, grad_fc2 = backward(
+        layer_in, grad_out, image, row, col, kept, count
+    )
+    starts, _ = offsets()
+    owned = [sums[s : s + m, :seg].reshape(-1) for s, m in zip(starts, SEG_ROWS)]
+    owned[FR] = owned[FR].reshape(-1, 2, HD // 2).sum(axis=1).reshape(-1)
+    return (
+        output,
+        grad_x,
+        owned[G1],
+        owned[B1],
+        grad_qkv,
+        owned[QB],
+        owned[FR],
+        grad_out_w,
+        owned[OB],
+        owned[G2],
+        owned[B2],
+        grad_fc1,
+        owned[F1B],
+        grad_fc2,
+        owned[F2B],
+    )
+
+
+def fits(mesh, tokens):
+    count, planes = mesh.shape["fsdp"], mesh.shape["dp"]
+    return count == 8 and planes == 4 and tokens == 640 * count * planes
+
+
 def solution(mesh):
     in_specs = (
         P(("fsdp", "dp"), None),
@@ -342,4 +1457,9 @@
         P("fsdp", None),
         P("fsdp"),
     )
-    return jax.shard_map(body, mesh=mesh, in_specs=in_specs, out_specs=out_specs, check_vma=False)
+    def step(*arguments):
+        chosen = fast_body if fits(mesh, arguments[0].shape[0]) else body
+        mapped = jax.shard_map(chosen, mesh=mesh, in_specs=in_specs, out_specs=out_specs, check_vma=False)
+        return mapped(*arguments)
+
+    return step

time: 988 us -> 238 us (0.24)
  waiting for transfers between devices: 551 us -> 0 us
  matrix products: 226 us -> 0 us
  Pallas kernels: 0 us -> 216 us
  blocking collectives: 109 us -> 0 us
  other arithmetic: 33.9 us -> 3.21 us
  local copies, waits for them, and re-layouts: 39.8 us -> 17.5 us
  between operations: 18 us -> 0.69 us
    reduce_scatter x4 -> x0, waiting for transfers between devices: 423 us -> none  [the longest x1 165 us: body(): lax.psum_scatter(grad_fc1, 'fsdp', scatter_dimension=0, tiled=True)]
    dot_general x96 -> x0, matrix products: 226 us -> none  [the longest x24 36.7 us: head_scores(): jnp.einsum('qd,kd->qk', query_one, key_one, preferred_element_type=jnp.fl...]
    pallas_call x0 -> x2, Pallas kernels: none -> 216 us  [the longest x1 120 us: backward(): pl.pallas_call(partial(backward_kernel, count, seg, shared, wide_shared),...]
    all_gather x4 -> x0, waiting for transfers between devices: 107 us -> none  [the longest x1 70.3 us: body(): lax.all_gather(fc2_weight, 'fsdp', axis=0, tiled=True)]
    unnamed x2 -> x0, blocking collectives: 76.2 us -> none
    all_gather x1 -> x0, blocking collectives: 26.7 us -> none  [body(): lax.all_gather(fc1_bias, 'fsdp', axis=0, tiled=True)]
    psum x1 -> x0, waiting for transfers between devices: 19 us -> none  [body(): lax.psum((owned[0], owned[1], owned[2], owned[3], owned[4], owned[5], own...]
    unnamed x109 -> x14, local copies, waits for them, and re-layouts: 26 us -> 8.28 us
  transfers between devices with their start and end apart: 9 -> 0, of which waited for: 6 -> 0; matrix products, arithmetic and copies ran while one was open for 27% -> 0% of each run, Pallas kernels for 0% -> 0%
where the time goes in v1:
time: 238 us; the launch traced here: 237 us
  Pallas kernels  216 us (91%)
  local copies, waits for them, and re-layouts  17.5 us (7%)
  other arithmetic  3.21 us (1%)
    pallas_call x1, Pallas kernels, backward(): pl.pallas_call(partial(backward_kernel, count, seg, shared, wide_shared),...  120 us
    pallas_call x1, Pallas kernels, forward(): pl.pallas_call(partial(forward_kernel, count, seg, shares), out_shape=[ja...  95.7 us
    unnamed x14, local copies, waits for them, and re-layouts  8.28 us

profile of v1, /device:TPU:0, one launch (start us, length us, event | category | flops | bytes accessed | tf_op | source)
XLA Modules:
  0.0 237.1 jit_solution(8438273477285122181)
XLA Ops:
  0.6 0.8 reshape.94
  1.4 0.7 broadcast_in_dim.7
  2.2 0.1 reshape.95
  2.2 0.8 reshape.99
  3.0 1.4 concatenate.3
  4.4 1.3 convert_bitcast_fusion.2.refs_1_.refs_2_
  5.7 0.6 pad_convert_fusion.refs_4_
  6.3 1.3 convert_bitcast_fusion
  7.6 95.7 %forward.1 = (bf16[640,768]{1,0:T(8,128)(2,1)}, f32[1,11520]{1,0:T(1,128)}, bf16[4,128,768]{2,1,0:T(8,128)(2,1)}, bf16[2304,640]{1,0:T(8,128)(2,1)}, bf16[640,76...) custom-call(bf16[640,768]{1,0:T(8,128)(2,1)} %refs_0_.3, ...), custom_call_target="tpu_custom_call" | custom-call | tf_op jit(solution)/shard_map/forward/pallas_call | solution.py:653
  103.3 120.0 %backward.1 = (bf16[640,768]{1,0:T(8,128)(2,1)}, f32[16,128]{1,0:T(8,128)}, f32[96,2304]{1,0:T(8,128)}, f32[96,768]{1,0:T(8,128)}, f32[96,3072]{1,0:T(8,128)}, /*index=5*/f32[384,768]{1,0:T(8,128)}) custom-call(bf16[640,768]{1,0:T(8,128)(2,1)} %refs_0_.3, bf16[640,768]{1,0:T(8,128)(2,1)} %refs_1_.1, f32[5,128]{1,0:T(8,128)} %convert_bitcast_fusion.2.refs_1_.refs_2_, ...), custom_call_target="tpu_custom_call" | custom-call | tf_op jit(solution)/shard_map/backward/pallas_call | solution.py:1035
  223.3 0.0 copy-start.2
  223.3 0.0 copy-start.3
  223.4 0.8 slice.30
  224.1 0.1 reshape_reshape.3
  224.2 0.6 reshape.104
  224.8 0.7 slice.29
  225.5 0.7 reshape.103
  226.2 0.7 slice.34
  226.8 1.3 slice_bitcast_fusion
  228.2 0.7 reshape.108
  228.8 0.0 copy-start.1
  228.8 2.3 copy.39
  231.1 0.0 copy-start
  231.1 2.3 copy.40
  233.4 0.0 copy-done.2
  233.5 0.9 copy.41
  234.4 0.0 copy-done.3
  234.4 0.7 copy.42
  235.1 0.0 copy-done.1
  235.1 1.0 copy.43
  236.1 0.0 copy-done
  236.1 1.0 copy.44
  (2 shorter events, 0.0 us)
Async XLA Ops:
  223.3 10.1 %copy-start.2 = (f32[96,2304]{1,0:T(8,128)S(1)}, f32[96,2304]{1,0:T(8,128)}, u32[]{:S(2)}) copy-start(f32[96,2304]{1,0:T(8,128)} %get-tuple-element.84) | copy-start | bytes 2654212
  223.3 11.0 %copy-start.3 = (f32[96,768]{1,0:T(8,128)S(1)}, f32[96,768]{1,0:T(8,128)}, u32[]{:S(2)}) copy-start(f32[96,768]{1,0:T(8,128)} %get-tuple-element.87) | copy-start | bytes 884740
  228.8 6.2 %copy-start.1 = (f32[96,3072]{1,0:T(8,128)S(1)}, f32[96,3072]{1,0:T(8,128)}, u32[]{:S(2)}) copy-start(f32[96,3072]{1,0:T(8,128)} %get-tuple-element.91) | copy-start | bytes 3538948
  231.1 5.0 %copy-start = (f32[384,768]{1,0:T(8,128)S(1)}, f32[384,768]{1,0:T(8,128)}, u32[]{:S(2)}) copy-start(f32[384,768]{1,0:T(8,128)} %get-tuple-element.93) | copy-start | bytes 3538948

commit v2 on v1

--- a/solution.py
+++ b/solution.py
@@ -278,6 +278,13 @@
             if i == 0:
                 self.ring_send(1)
 
+    def go(self, step):
+        if step == 0:
+            self.add_other(0, 1)
+            return
+        self.add_other(2 * step - 1, 2 * step + 1)
+        self.ring_step(step)
+
     def ring_send(self, step):
         for direction in range(2):
             self.ring_out[direction, step].start()
@@ -322,6 +329,49 @@
         self.out_in.wait_recv()
         for copy in self.other_out + list(self.ring_out.values()) + [self.final_out, self.out_out]:
             copy.wait_send()
+
+
+FORWARD_ORDER = {
+    "entry": ((1, 0), (0, 0),),
+    "bias": ((2, 0), (1, 1), (0, 1), (2, 1),),
+    "norm": ((1, 2), (0, 2), (3, 0), (1, 3), (2, 2), (0, 3), (4, 0), (3, 1), (1, 4), (5, 0), (0, 4), (6, 0),),
+    "tables": ((1, 5), (0, 5), (1, 6), (2, 3), (3, 2), (0, 6),),
+    "q": ((5, 1), (4, 1),),
+    "k": ((2, 4), (6, 1),),
+    "v": ((3, 3),),
+    "pair1": ((5, 2),),
+    "pair2": ((2, 5),),
+    "pair3": ((2, 6), (4, 2), (3, 4),),
+    "pair4": ((6, 2),),
+    "pair5": ((4, 3), (5, 3),),
+    "mix": ((3, 5),),
+    "norm2": ((3, 6), (4, 4), (6, 3),),
+    "hid1": ((4, 5), (5, 4), (6, 4), (4, 6),),
+    "hid2": ((5, 5),),
+    "hid3": ((5, 6),),
+    "res0": ((6, 5),),
+    "res1": ((6, 6),),
+}
+BACKWARD_ORDER = {
+    "hid1": ((8, -1),),
+    "hid3": ((8, -2),),
+    "dw1_2": ((8, 0),),
+    "dw1_3": ((0, -1), (1, -1), (2, -1),),
+    "ng1": ((8, 1), (0, 0),),
+    "nb2": ((1, 0), (3, -1),),
+    "mixb": ((0, 1), (8, 2), (2, 0),),
+    "bias": ((3, 0), (1, 1), (4, -1),),
+    "pair0": ((4, 0),),
+    "pair1": ((8, 3), (3, 1), (0, 2),),
+    "pair3": ((4, 1), (2, 1), (5, -1), (3, 2), (1, 2),),
+    "pair4": ((5, 0), (8, 4), (6, -1), (2, 2), (4, 2), (0, 3),),
+    "pair5": ((5, 1),),
+    "ox0": ((1, 3), (6, 0), (7, -1), (4, 3),),
+    "ox1": ((3, 3),),
+    "ox2": ((7, 0), (6, 1), (2, 3),),
+    "nb1": ((7, 1), (1, 4), (0, 4), (6, 2),),
+    "pack": ((5, 2), (9, 0), (3, 4), (7, 2), (2, 4), (9, 1), (6, 3), (1, 5), (4, 4), (5, 3), (0, 5), (7, 3), (8, 5), (2, 5), (6, 4), (9, 2), (3, 5), (5, 4), (4, 5), (7, 4), (6, 5), (9, 3), (5, 5), (7, 5),),
+}
 
 
 SEG_ROWS = (1, 1, 3, 2, 1, 1, 1, 4, 1)
@@ -443,7 +493,7 @@
     return lax.dot_general(left, right, (((1,), (1,)), ((), ())), preferred_element_type=jnp.float32)
 
 
-def project(normed_low, weights, vec, cosine, sine, outs):
+def project(normed_low, weights, vec, cosine, sine, outs, at):
     tile = 256
     per = D // tile
     for which, out in enumerate(outs):
@@ -460,6 +510,7 @@
             out[:, cols] = t.astype(jnp.bfloat16)
 
         loop(per, body)
+        at("qkv"[which])
 
 
 def attend(pair, query, key, value, bias, mixed, lse, block):
@@ -531,7 +582,7 @@
     output[:, cols] = (middle[:, cols] + matmul(active[...], weights[:, cols]) + shift).astype(jnp.bfloat16)
 
 
-def forward_kernel(count, seg, shares, *refs):
+def forward_kernel(count, seg, *refs):
     (x, image, row, col, small, qkv_s, out_s, fc1_s, fc2_s) = refs[:9]
     (output, vec_o, tables_o, turned_o, q_o, k_o, v_o, lse_o, middle_o, act_t_o, slope_o,
      qkv_o, out_o, fc1_o, fc2_o) = refs[9:24]
@@ -543,22 +594,31 @@
     peers = [(lax.rem(where.fsdp + i, count), where.dp) for i in range(1, count)]
     where.greet(peers)
     sems = Sems(send, recv)
+    cuts = (
+        (qkv_s, qkv_w, 0, 1280), (qkv_s, qkv_w, 1280, 1024), (out_s, out_w, 0, D),
+        (fc1_s, fc1_w, 0, MLP // 2), (fc1_s, fc1_w, MLP // 2, MLP // 2), (fc2_s, fc2_w, 0, 512), (fc2_s, fc2_w, 512, 256),
+    )
     flows = [
-        Gather(where, sems, s, w, shared, local.at[i])
-        for i, (s, w, shared) in enumerate(
-            zip((qkv_s, out_s, fc1_s, fc2_s), (qkv_w, out_w, fc1_w, fc2_w), shares)
-        )
+        Gather(where, sems, s.at[:, pl.ds(at, size)], w.at[:, pl.ds(at, size)], s.shape[0] // 3, local.at[i])
+        for i, (s, w, at, size) in enumerate(cuts)
     ]
-    qkv_f, out_f, fc1_f, fc2_f = flows
-    far = where.far
+
+    def at(point):
+        for i, step in FORWARD_ORDER.get(point, ()):
+            if step == 0:
+                flows[i].start()
+            elif step <= where.far + 1:
+                flows[i].tick(step)
+            else:
+                flows[i].finish()
+
     small_copies = [
         remote(small, slots.at[where.fsdp], (small_send.at[i], small_recv.at[i]), peers[i])
         for i in range(count - 1)
     ]
     for copy in small_copies:
         copy.start()
-    qkv_f.start()
-    out_f.start()
+    at("entry")
     slots[where.fsdp] = small[...]
     saves = []
 
@@ -573,57 +633,49 @@
         remote(came, came, (small_send.at[i - 1], small_recv.at[i - 1]), peers[i - 1]).wait_recv()
     unpack_small(slots, vec, count, seg)
     save(vec, vec_o)
+    at("bias")
     norm_rows(x, n1, vec, G1, B1)
     turn(n1, turned)
-    qkv_f.tick(1)
-    fc1_f.start()
-    out_f.tick(1)
+    lse[...] = jnp.zeros_like(lse)
+    at("norm")
     rope_tables(vec, col, row, cosine, sine, tables)
     save(tables, tables_o)
-    lse[...] = jnp.zeros_like(lse)
-    for step in range(2, far + 2):
-        qkv_f.tick(step)
-        out_f.tick(step)
-        if step == 3:
-            fc2_f.start()
-            fc1_f.tick(1)
-    qkv_f.finish()
-    project(n1, qkv_w, vec, cosine, sine, (q, k, v))
-    out_f.finish()
+    at("tables")
+    project(n1, qkv_w, vec, cosine, sine, (q, k, v), at)
     save(qkv_w, qkv_o)
-    save(out_w, out_o)
     save(q, q_o)
     save(k, k_o)
     save(v, v_o)
 
-    ticks = [(fc2_f, 1), (fc1_f, 2), (fc2_f, 2), (fc1_f, 3), (fc2_f, 3), (fc1_f, 4), (fc2_f, 4), (fc1_f, 5)]
-    ticks = ticks if far == 4 else []
-
     def pair_body(j):
         attend(j, q, k, v, bias, mixed, lse, 320)
-        for i, (flow, step) in enumerate(ticks):
-            @pl.when(j == min(i // 2 + 1, 5))
-            def _(flow=flow, step=step):
-                flow.tick(step)
+        for i in range(H // 2):
+            @pl.when(j == i)
+            def _(i=i):
+                at(f"pair{i}")
 
     loop(H // 2, pair_body)
     lse_t[...] = lse[...].T
     save(lse_t, lse_o)
     turn(mixed, turned, D)
+    save(out_w, out_o)
     mix_out(x, mixed, out_w, vec, middle)
     save(middle, middle_o)
+    at("mix")
     norm_rows(middle, n2, vec, G2, B2)
     turn(n2, turned, 2 * D)
     save(turned, turned_o)
-    fc2_f.tick(far + 1)
-    fc1_f.finish()
-    loop(MLP // 256, lambda j: hidden_tile(j, n2, fc1_w, vec, act, act_t, slope))
+    at("norm2")
+    for i in range(4):
+        loop(MLP // 1024, lambda j: hidden_tile(MLP // 1024 * i + j, n2, fc1_w, vec, act, act_t, slope))
+        at(f"hid{i}")
     save(act_t, act_t_o)
     save(slope, slope_o)
     save(fc1_w, fc1_o)
-    fc2_f.finish()
+    for i in range(D // 256):
+        result_tile(i, middle, act, fc2_w, vec, output)
+        at(f"res{i}")
     save(fc2_w, fc2_o)
-    loop(D // 256, lambda j: result_tile(j, middle, act, fc2_w, vec, output))
     for flow in flows:
         flow.drain()
     for copy in small_copies:
@@ -636,7 +688,6 @@
     bf16, f32 = jnp.bfloat16, jnp.float32
     tokens = x.shape[0]
     seg = D // count
-    shares = tuple(w.shape[0] // 3 for w in weights)
     wide = lambda kind, width=D: ((tokens, width), kind)
     total = offsets()[1] * D
     full = [((w.shape[0] * count, w.shape[1]), bf16) for w in weights]
@@ -644,14 +695,14 @@
         ((1, total), f32), ((4, 128, D), bf16), ((3 * D, tokens), bf16), wide(bf16), wide(bf16), wide(bf16),
         ((128, tokens), f32), wide(f32), ((MLP, tokens), bf16), wide(bf16, MLP),
     ] + full
-    copies = 4 * 8 * (count // 2)
+    copies = 7 * 8 * (count // 2)
     any_spec = pl.BlockSpec(memory_space=pl.ANY)
     vmem_spec = pl.BlockSpec(memory_space=pltpu.VMEM)
     scratch = kept + [
         wide(f32), wide(f32), ((tokens, tokens), f32), wide(f32, 128), wide(bf16, MLP), wide(bf16),
     ]
     return pl.pallas_call(
-        partial(forward_kernel, count, seg, shares),
+        partial(forward_kernel, count, seg),
         out_shape=[jax.ShapeDtypeStruct((tokens, D), bf16)] + [jax.ShapeDtypeStruct(*s) for s in kept],
         in_specs=[vmem_spec] * 9,
         out_specs=[vmem_spec] + [any_spec] * len(kept),
@@ -662,7 +713,7 @@
             pltpu.SemaphoreType.DMA((copies,)),
             pltpu.SemaphoreType.DMA((count - 1,)),
             pltpu.SemaphoreType.DMA((count - 1,)),
-            pltpu.SemaphoreType.DMA((4,)),
+            pltpu.SemaphoreType.DMA((7,)),
             pltpu.SemaphoreType.DMA((len(kept),)),
         ],
         compiler_params=pltpu.CompilerParams(
@@ -767,7 +818,7 @@
                 slots[f, first + i : first + i + 1, :] = jnp.where(lane < seg, row, 0.0)
 
 
-def backward_kernel(count, seg, shared, wide_shared, *refs):
+def backward_kernel(count, seg, shares, wide_shared, *refs):
     (x, grad_out, image, row, col, vec_h, tables_h, turned_h, q_h, k_h, v_h, lse_h, middle_h, act_t_h, slope_h,
      qkv_h, out_h, fc1_h, fc2_h) = refs[:19]
     (grad_x, small_out, grad_qkv, grad_out_w, grad_fc1, grad_fc2) = refs[19:25]
@@ -789,14 +840,6 @@
         loads[name] = copy
 
     load("act", act_t_h, act_t)
-    load("fc2", fc2_h, fc2_w)
-    load("slope", slope_h, slope)
-    load("fc1", fc1_h, fc1_w)
-    for name, source, target in (
-        ("vec", vec_h, vec), ("middle", middle_h, middle), ("out", out_h, out_w), ("q", q_h, q), ("k", k_h, k),
-        ("v", v_h, v), ("lse", lse_h, lse_t), ("tables", tables_h, tables),
-    ):
-        load(name, source, target)
     peers = [(lax.rem(where.fsdp + i, count), where.dp) for i in range(1, count)]
     where.greet(peers)
     sems = Sems(send, recv)
@@ -804,12 +847,14 @@
     parts = [
         Reduce(
             where, sems, big.at[pl.ds(D * (i % 4), D)], grad_out_w if i == 4 else outs[i - (i > 4)],
-            shared, bufs[4 + 4 * i : 8 + 4 * i],
+            shares[i], bufs[4 + 4 * i : 8 + 4 * i],
         )
         for i in range(8)
     ]
 
     loads["act"].wait()
+    load("fc2", fc2_h, fc2_w)
+    load("slope", slope_h, slope)
     loop(8, lambda i: store_tile(big, i, 384, act_t, grad_out))
     fc2.start()
     at = starts[F2B] * D
@@ -817,6 +862,12 @@
     loads["fc2"].wait()
     loads["slope"].wait()
     load("turned", turned_h, act_t.at[pl.ds(0, 3 * D)])
+    load("fc1", fc1_h, fc1_w)
+    for name, source, target in (
+        ("vec", vec_h, vec), ("middle", middle_h, middle), ("out", out_h, out_w), ("q", q_h, q), ("k", k_h, k),
+        ("v", v_h, v), ("lse", lse_h, lse_t), ("tables", tables_h, tables),
+    ):
+        load(name, source, target)
     normed_one, mixed_t, normed_two = (act_t.at[pl.ds(D * i, D)] for i in range(3))
 
     def hidden(j):
@@ -827,41 +878,73 @@
         at = pl.ds(pl.multiple_of(starts[F1B] * D + 256 * j, 256), 256)
         sums[:, at] = jnp.sum(g.astype(f32), axis=0, keepdims=True)
 
-    loop(MLP // 256, hidden)
-    fc2.add_pair()
+    take = lambda i: (small_send.at[i], small_recv.at[i])
+    to_twin = remote(slots, slots_twin, take(0), where.twin)
+    to_across = remote(slots, slots_across, take(1), where.across)
+    given = [
+        remote(slots.at[peer[0]], slots_in.at[where.fsdp], take(2 + i), peer) for i, peer in enumerate(peers)
+    ]
+    every = parts + [fc2]
+
+    def small_step(step):
+        if step == 0:
+            to_twin.start()
+        elif step == 1:
+            to_twin.wait()
+            slots[...] = slots[...] + slots_twin[...]
+            to_across.start()
+        elif step == 2:
+            to_across.wait()
+            slots[...] = slots[...] + slots_across[...]
+            slots_in[where.fsdp] = slots[where.fsdp]
+            for copy in given:
+                copy.start()
+        else:
+            for i in range(1, count):
+                came = slots_in.at[lax.rem(where.fsdp + count - i, count)]
+                remote(came, came, take(1 + i), peers[i - 1]).wait_recv()
+            total = slots_in[0]
+            for i in range(1, count):
+                total = total + slots_in[i]
+            small_out[...] = total
+
+    def reach(point):
+        for i, step in BACKWARD_ORDER.get(point, ()):
+            if i == 9:
+                small_step(step)
+            elif step < 0:
+                bounds = ((0, None),) if i < 8 else ((0, 3), (3, None))
+                every[i].add_pair(*bounds[-1 - step])
+            elif step <= far:
+                every[i].go(step)
+            else:
+                every[i].finish()
+
+    reach("dw2")
+    for i in range(4):
+        loop(MLP // 1024, lambda j: hidden(MLP // 1024 * i + j))
+        reach(f"hid{i}")
     fc2.sent_pair()
     loads["turned"].wait()
     for i in range(4):
         grad_part = slope.at[:, pl.ds(D * i, D)]
         loop(2, lambda j: store_tile(big.at[pl.ds(D * i, D)], j, 384, normed_two, grad_part))
         parts[i].start()
-        if i:
-            parts[i - 1].add_pair()
-        if i == 1:
-            fc2.add_other()
-        if i == 3:
-            fc2.ring_step(1)
+        reach(f"dw1_{i}")
     loads["fc1"].wait()
 
     def normed_grad(j):
         cols = tile_at(j, 256)
         wide[:, cols] = matmul_nt(slope[...], fc1_w[cols, :])
 
-    normed_grad(0)
-    parts[3].add_pair()
-    parts[0].add_other()
-    normed_grad(1)
-    parts[1].add_other()
-    fc2.ring_step(2)
-    parts[0].ring_step(1)
-    normed_grad(2)
+    for i in range(3):
+        normed_grad(i)
+        reach(f"ng{i}")
     for i in range(4):
         parts[i].sent_pair()
     load("qkv", qkv_h, big_rows(fc1_w))
     loads["vec"].wait()
     loads["middle"].wait()
-    parts[2].add_other()
-    parts[1].ring_step(1)
 
     at = starts[OB] * D
     sums[:, at : at + D] = jnp.zeros((1, D), f32)
@@ -873,12 +956,10 @@
         sums[:, at : at + D] += jnp.sum(total.astype(f32), axis=0, keepdims=True)
 
     norm_back(middle, wide, grad_out, G2, vec, sums, G2, B2, keep_middle)
-    parts[3].add_other()
-    fc2.ring_step(3)
-    parts[0].ring_step(2)
-    parts[2].ring_step(1)
+    reach("nb2")
     loop(2, lambda j: store_tile(big.at[pl.ds(0, D)], j, 384, mixed_t, low))
     parts[4].start()
+    reach("dwo")
     loads["out"].wait()
     mixed_grad = slope.at[:, pl.ds(3 * D, D)]
 
@@ -887,7 +968,7 @@
         mixed_grad[:, cols] = matmul_nt(low[...], out_w[cols, :]).astype(bf16)
 
     loop(D // 256, mix_back)
-    parts[4].add_pair()
+    reach("mixb")
 
     image_bias(image, bias)
     lane = lax.broadcasted_iota(jnp.int32, (128, 128), 1)
@@ -901,19 +982,7 @@
     for name in ("q", "k", "v", "lse", "tables"):
         loads[name].wait()
 
-    turns = {
-        0: [lambda: parts[3].ring_step(1), lambda: fc2.ring_step(4), lambda: parts[0].ring_step(3),
-            lambda: parts[1].ring_step(2), lambda: parts[4].add_other()],
-        1: [lambda: parts[2].ring_step(2), lambda: parts[0].ring_step(4), lambda: parts[3].ring_step(2),
-            lambda: parts[1].ring_step(3), lambda: parts[4].ring_step(1)],
-        2: [lambda: fc2.finish(), lambda: parts[2].ring_step(3), lambda: parts[1].ring_step(4),
-            lambda: parts[3].ring_step(3), lambda: parts[4].ring_step(2), lambda: parts[5].add_pair()],
-        3: [lambda: parts[0].finish(), lambda: parts[2].ring_step(4), lambda: parts[3].ring_step(4),
-            lambda: parts[4].ring_step(3), lambda: parts[5].add_other()],
-        4: [lambda: parts[1].finish(), lambda: parts[4].ring_step(4), lambda: parts[5].ring_step(1),
-            lambda: parts[6].add_pair()],
-        5: [lambda: parts[2].finish(), lambda: parts[5].ring_step(2), lambda: parts[6].add_other()],
-    }
+    reach("bias")
     tokens = q.shape[0]
     blocks = [(i, min(256, tokens - i)) for i in range(0, tokens, 256)]
 
@@ -921,71 +990,32 @@
         attend_back(
             j, q, k, v, lse_t, bias, tables, pick_col, pick_row, colb, rowb, mixed_grad, slope, sums, blocks
         )
-        for i, steps in turns.items():
+        for i in range(H // 2):
             @pl.when(j == i)
-            def _(i=i, steps=steps):
+            def _(i=i):
                 if i % 2:
                     project_back(parts[5 + i // 2].grad, normed_one, slope, i // 2)
                     parts[5 + i // 2].start()
-                for step in steps:
-                    step()
+                reach(f"pair{i}")
 
     loop(H // 2, pair_body)
     loads["qkv"].wait()
     qkv_w = big_rows(fc1_w)
-    parts[7].add_pair()
-    parts[5].ring_step(3)
-    parts[6].ring_step(1)
-
     def normed_one_grad(j):
         cols = tile_at(j, 256)
         middle[:, cols] = matmul_nt(slope[:, pl.ds(0, 3 * D)], qkv_w[cols, :])
 
-    normed_one_grad(0)
-    parts[7].add_other()
-    parts[5].ring_step(4)
-    parts[6].ring_step(2)
-    normed_one_grad(1)
-    parts[7].ring_step(1)
-    parts[6].ring_step(3)
-    parts[3].finish()
-    normed_one_grad(2)
-    parts[7].ring_step(2)
-    parts[6].ring_step(4)
-    parts[4].finish()
+    for i in range(3):
+        normed_one_grad(i)
+        reach(f"ox{i}")
 
     def keep_x(rows, total):
         grad_x[rows, :] = total.astype(bf16)
 
     norm_back(x, middle, wide, G1, vec, sums, G1, B1, keep_x)
-    parts[7].ring_step(3)
+    reach("nb1")
     pack_sums(sums, slots, count, seg)
-    take = lambda i: (small_send.at[i], small_recv.at[i])
-    to_twin = remote(slots, slots_twin, take(0), where.twin)
-    to_twin.start()
-    parts[5].finish()
-    parts[7].ring_step(4)
-    to_twin.wait()
-    slots[...] = slots[...] + slots_twin[...]
-    to_across = remote(slots, slots_across, take(1), where.across)
-    to_across.start()
-    parts[6].finish()
-    to_across.wait()
-    slots[...] = slots[...] + slots_across[...]
-    slots_in[where.fsdp] = slots[where.fsdp]
-    given = [
-        remote(slots.at[peer[0]], slots_in.at[where.fsdp], take(2 + i), peer) for i, peer in enumerate(peers)
-    ]
-    for copy in given:
-        copy.start()
-    parts[7].finish()
-    for i in range(1, count):
-        came = slots_in.at[lax.rem(where.fsdp + count - i, count)]
-        remote(came, came, take(1 + i), peers[i - 1]).wait_recv()
-    total = slots_in[0]
-    for i in range(1, count):
-        total = total + slots_in[i]
-    small_out[...] = total
+    reach("pack")
     for copy in given:
         copy.wait_send()
     for i in range(4, 8):
@@ -1018,7 +1048,7 @@
     bf16, f32 = jnp.bfloat16, jnp.float32
     tokens = x.shape[0]
     seg = D // count
-    shared, wide_shared = seg // 96 * 16, seg
+    shares, wide_shared = tuple(16 + 16 * (i % 2) for i in range(8)), seg
     (vec, tables, turned, q, k, v, lse, middle, act_t, slope, qkv, out, fc1, fc2) = kept
     like = lambda a: pltpu.VMEM(a.shape, a.dtype)
     side = pltpu.VMEM((tokens, 128), f32)
@@ -1026,14 +1056,14 @@
     slots = pltpu.VMEM((count, 16, 128), f32)
     part = pltpu.VMEM((seg, D), f32)
     flows = Reduce.shapes(MLP // count, D, count, wide_shared)
-    for _ in range(8):
+    for shared in shares:
         flows = flows + Reduce.shapes(seg, D, count, shared)
     copies = 9 * Reduce.copies(count)
     any_spec = pl.BlockSpec(memory_space=pl.ANY)
     vmem_spec = pl.BlockSpec(memory_space=pltpu.VMEM)
     dma = pltpu.SemaphoreType.DMA
     return pl.pallas_call(
-        partial(backward_kernel, count, seg, shared, wide_shared),
+        partial(backward_kernel, count, seg, shares, wide_shared),
         out_shape=[
             jax.ShapeDtypeStruct((tokens, D), bf16),
             jax.ShapeDtypeStruct((16, 128), f32),

time: 238 us -> 207 us (0.87); the launches traced: 237 us -> 203 us
  Pallas kernels: 216 us -> 182 us
    pallas_call x2, Pallas kernels: 216 us -> 182 us  [the longest x1 94.2 us: backward(): pl.pallas_call(partial(backward_kernel, count, seg, shares, wide_shared),...]
where the time goes in v2:
time: 207 us; the launch traced here: 203 us
  Pallas kernels  182 us (88%)
  local copies, waits for them, and re-layouts  17.5 us (8%)
  other arithmetic  3.21 us (2%)
    pallas_call x1, Pallas kernels, backward(): pl.pallas_call(partial(backward_kernel, count, seg, shares, wide_shared),...  94.2 us
    pallas_call x1, Pallas kernels, forward(): pl.pallas_call(partial(forward_kernel, count, seg), out_shape=[jax.ShapeD...  87.3 us
    unnamed x14, local copies, waits for them, and re-layouts  8.28 us

profile of v2, /device:TPU:0, one launch (start us, length us, event | category | flops | bytes accessed | tf_op | source)
XLA Modules:
  0.0 203.4 jit_solution(4041840162306198099)
XLA Ops:
  0.6 0.8 reshape.94
  1.4 0.7 broadcast_in_dim.7
  2.2 0.1 reshape.95
  2.2 0.8 reshape.99
  3.0 1.4 concatenate.3
  4.4 1.3 convert_bitcast_fusion.2.refs_1_.refs_2_
  5.7 0.6 pad_convert_fusion.refs_4_
  6.3 1.3 convert_bitcast_fusion
  7.6 87.3 %forward.1 = (bf16[640,768]{1,0:T(8,128)(2,1)}, f32[1,11520]{1,0:T(1,128)}, bf16[4,128,768]{2,1,0:T(8,128)(2,1)}, bf16[2304,640]{1,0:T(8,128)(2,1)}, bf16[640,76...) custom-call(bf16[640,768]{1,0:T(8,128)(2,1)} %refs_0_.3, ...), custom_call_target="tpu_custom_call" | custom-call | tf_op jit(solution)/shard_map/forward/pallas_call | solution.py:704
  95.0 94.2 %backward.1 = (bf16[640,768]{1,0:T(8,128)(2,1)}, f32[16,128]{1,0:T(8,128)}, f32[96,2304]{1,0:T(8,128)}, f32[96,768]{1,0:T(8,128)}, f32[96,3072]{1,0:T(8,128)}, /*index=5*/f32[384,768]{1,0:T(8,128)}) custom-call(bf16[640,768]{1,0:T(8,128)(2,1)} %refs_0_.3, bf16[640,768]{1,0:T(8,128)(2,1)} %refs_1_.1, f32[5,128]{1,0:T(8,128)} %convert_bitcast_fusion.2.refs_1_.refs_2_, ...), custom_call_target="tpu_custom_call" | custom-call | tf_op jit(solution)/shard_map/backward/pallas_call | solution.py:1065
  189.2 0.0 copy-start.2
  189.2 0.0 copy-start.3
  189.2 0.8 slice.30
  190.0 0.1 reshape_reshape.3
  190.1 0.6 reshape.104
  190.7 0.7 slice.29
  191.3 0.7 reshape.103
  192.0 0.7 slice.34
  192.7 1.3 slice_bitcast_fusion
  194.0 0.7 reshape.108
  194.7 0.0 copy-start.1
  194.7 2.3 %copy.39 = bf16[640,768]{1,0:T(8,128)(2,1)} copy(bf16[640,768]{1,0:T(8,128)(2,1)} %get-tuple-element.80) | data formatting | bytes 1966080
  197.0 0.0 copy-start
  197.0 2.3 %copy.40 = bf16[640,768]{1,0:T(8,128)(2,1)} copy(bf16[640,768]{1,0:T(8,128)(2,1)} %get-tuple-element.81) | data formatting | bytes 1966080
  199.3 0.0 copy-done.2
  199.3 0.9 copy.41
  200.2 0.0 copy-done.3
  200.2 0.7 copy.42
  200.9 0.0 copy-done.1
  200.9 1.0 copy.43
  201.9 0.0 copy-done
  201.9 1.0 copy.44
  (2 shorter events, 0.0 us)
Async XLA Ops:
  189.2 10.1 %copy-start.2 = (f32[96,2304]{1,0:T(8,128)S(1)}, f32[96,2304]{1,0:T(8,128)}, u32[]{:S(2)}) copy-start(f32[96,2304]{1,0:T(8,128)} %get-tuple-element.84) | copy-start | bytes 2654212
  189.2 11.0 %copy-start.3 = (f32[96,768]{1,0:T(8,128)S(1)}, f32[96,768]{1,0:T(8,128)}, u32[]{:S(2)}) copy-start(f32[96,768]{1,0:T(8,128)} %get-tuple-element.87) | copy-start | bytes 884740
  194.7 6.2 %copy-start.1 = (f32[96,3072]{1,0:T(8,128)S(1)}, f32[96,3072]{1,0:T(8,128)}, u32[]{:S(2)}) copy-start(f32[96,3072]{1,0:T(8,128)} %get-tuple-element.91) | copy-start | bytes 3538948
  197.0 5.0 %copy-start = (f32[384,768]{1,0:T(8,128)S(1)}, f32[384,768]{1,0:T(8,128)}, u32[]{:S(2)}) copy-start(f32[384,768]{1,0:T(8,128)} %get-tuple-element.93) | copy-start | bytes 3538948
